TPU v7x, 32 devices: a whole 2x2x4 slice. The times are simulated.
32 devices in a mesh: row: 4 (over x, core), col: 8 (over z, y).
Axes of the slice: x: 2, y: 2, z: 4, core: 2. Of those that a mesh axis runs over, the one named last changes fastest.
Arguments:
- rhs: float32 [4, 8, 8, 4, 128], P('row', 'col'), may hold values from -6 to 6
- diag0: float32 [4, 8, 8, 128], P('row', 'col'), may hold values from 2 to 4
- blocks0: float32 [4, 8, 8, 14, 128, 128], P('row', 'col'), may hold values from -0.1875 to 0.1875
- cols0: int32 [4, 8, 8, 14], P('row', 'col'), may hold values from 0 to 23
- sends0: int32 [4, 8, 4, 4], P('row', 'col'), may hold values from 0 to 7
- pro0: float32 [4, 8, 8, 128, 128], P('row', 'col'), may hold values from -0.5 to 0.5
- agg0: int32 [4, 8, 8], P('row', 'col'), may hold values from 0 to 1
- diag1: float32 [4, 8, 2, 128], P('row', 'col'), may hold values from 2 to 4
- blocks1: float32 [4, 8, 2, 14, 128, 128], P('row', 'col'), may hold values from -0.1875 to 0.1875
- cols1: int32 [4, 8, 2, 14], P('row', 'col'), may hold values from 0 to 9
- sends1: int32 [4, 8, 4, 2], P('row', 'col'), may hold values from 0 to 1
- pro1: float32 [4, 8, 2, 128, 128], P('row', 'col'), may hold values from -0.25 to 0.25
- agg1: int32 [4, 8, 2], P('row', 'col'), may hold values from 0 to 7
- cinv: float32 [1024, 1024], P(('row', 'col')), may hold values from -0.1875 to 0.1875
Outputs:
- solution: float32 [4, 8, 8, 4, 128], P('row', 'col')
Inputs may be any that keep to these rules, and one draw needn't show every extreme that they name: `sends0`: indices of the sender's own fine blocks. `sends1`: indices of the sender's own level-one blocks. `cols0`: indices into the extended fine vector of 24 blocks. `cols1`: indices into the extended level-one vector of 10 blocks. `agg0`: a level-one block of the same partition. `agg1`: a coarsest block, on any partition.
All inputs are finite; a program needn't handle non-finite values.
Results may differ from a plain program's by a relative error of at most 0.0001.
Values sent between devices are 32-bit elements; how exact they have to be, the bound alone decides.
No kernel may reach another device: no remote copies, remote signals or barrier semaphores. Data moves between devices by JAX's collectives and lax.ppermute only.
A program may use at most 64 MiB of HBM per device.

v0:
```python
import jax
import jax.numpy as jnp
from jax import lax
from jax.sharding import PartitionSpec as P

NU = 2
HIGH = lax.Precision.HIGHEST
OMEGA = 0.3


def padded_2(value, sides, width):
    for axis, dim in sides:
        size, length = (lax.axis_size(axis), value.shape[dim])
        up = [(i, (i + 1) % size) for i in range(size - 1)]
        down = [(j, i) for i, j in up]
        last = lax.slice_in_dim(value, length - width, length, axis=dim)
        leading = lax.slice_in_dim(value, 0, width, axis=dim)
        before = lax.ppermute(last, axis, up)
        after = lax.ppermute(leading, axis, down)
        value = jnp.concatenate([before, value, after], axis=dim)
    return value


def gather_ghosts(vector, sends):
    packed = vector[sends]
    padded = padded_2(packed[None, None], (("row", 0), ("col", 1)), 1)
    return jnp.concatenate(
        [vector, padded[0, 1, 0], padded[2, 1, 1], padded[1, 0, 2], padded[1, 2, 3]], axis=0
    )


def apply_op(vector, diag, blocks, cols, sends):
    extended = gather_ghosts(vector, sends)
    nearby = extended[cols]
    coupled = jnp.einsum("bkij,bkrj->bri", blocks, nearby, precision=HIGH)
    return diag[:, None, :] * vector + coupled


def smooth(vector, right_side, diag, blocks, cols, sends, count):
    for sweep in range(count):
        vector = (
            vector
            + OMEGA * (right_side - apply_op(vector, diag, blocks, cols, sends)) / diag[:, None, :]
        )
    return vector


def on_device(
    rhs, diag0, blocks0, cols0, sends0, pro0, agg0, diag1, blocks1, cols1, sends1, pro1, agg1, cinv
):
    fine_rhs = rhs[0, 0]
    fine_diag = diag0[0, 0]
    fine_blocks = blocks0[0, 0]
    fine_cols = cols0[0, 0]
    fine_sends = sends0[0, 0]
    fine_pro = pro0[0, 0]
    level_diag = diag1[0, 0]
    level_blocks = blocks1[0, 0]
    level_cols = cols1[0, 0]
    level_sends = sends1[0, 0]
    level_pro = pro1[0, 0]
    level_count = level_diag.shape[0]
    block_size = level_diag.shape[1]
    loads = fine_rhs.shape[1]
    coarse_total = cinv.shape[1]
    coarse_count = coarse_total // block_size
    fine_x = OMEGA * fine_rhs / fine_diag[:, None, :]
    fine_x = smooth(fine_x, fine_rhs, fine_diag, fine_blocks, fine_cols, fine_sends, NU - 1)
    fine_res = fine_rhs - apply_op(fine_x, fine_diag, fine_blocks, fine_cols, fine_sends)
    onehot0 = (agg0[0, 0][:, None] == jnp.arange(level_count)).astype(jnp.float32)
    restricted = jnp.einsum("bij,bri->brj", fine_pro, fine_res, precision=HIGH)
    level_rhs = jnp.einsum("bc,brj->crj", onehot0, restricted, precision=HIGH)
    level_x = OMEGA * level_rhs / level_diag[:, None, :]
    level_x = smooth(level_x, level_rhs, level_diag, level_blocks, level_cols, level_sends, NU - 1)
    level_res = level_rhs - apply_op(level_x, level_diag, level_blocks, level_cols, level_sends)
    onehot1 = (agg1[0, 0][:, None] == jnp.arange(coarse_count)).astype(jnp.float32)
    contrib = jnp.einsum("bij,bri->brj", level_pro, level_res, precision=HIGH)
    term = jnp.einsum("bc,brj->rcj", onehot1, contrib, precision=HIGH).reshape(loads, coarse_total)
    coarse_rhs = lax.psum(term, ("row", "col"))
    own_rows = jnp.einsum("ij,rj->ri", cinv, coarse_rhs, precision=HIGH)
    coarse_x = lax.all_gather(own_rows, ("row", "col"), axis=1, tiled=True)
    coarse_blocks = coarse_x.reshape(loads, coarse_count, block_size)
    picked = jnp.einsum("bc,rcj->brj", onehot1, coarse_blocks, precision=HIGH)
    level_x = level_x + jnp.einsum("bij,brj->bri", level_pro, picked, precision=HIGH)
    level_x = smooth(level_x, level_rhs, level_diag, level_blocks, level_cols, level_sends, NU)
    lifted = jnp.einsum("bc,crj->brj", onehot0, level_x, precision=HIGH)
    fine_x = fine_x + jnp.einsum("bij,brj->bri", fine_pro, lifted, precision=HIGH)
    fine_x = smooth(fine_x, fine_rhs, fine_diag, fine_blocks, fine_cols, fine_sends, NU)
    return fine_x[None, None]


def solution(mesh):
    return jax.shard_map(
        on_device,
        mesh=mesh,
        in_specs=(
            P("row", "col", None, None, None),
            P("row", "col", None, None),
            P("row", "col", None, None, None, None),
            P("row", "col", None, None),
            P("row", "col", None, None),
            P("row", "col", None, None, None),
            P("row", "col", None),
            P("row", "col", None, None),
            P("row", "col", None, None, None, None),
            P("row", "col", None, None),
            P("row", "col", None, None),
            P("row", "col", None, None, None),
            P("row", "col", None),
            P(("row", "col"), None),
        ),
        out_specs=P("row", "col", None, None, None),
        check_vma=False,
    )
```

profile of v0, /device:TPU:1, one launch (start us, length us, event | category | flops | bytes accessed | tf_op | source)
XLA Modules:
  0.0 297.1 jit_solution(16686773013737030327)
XLA Ops:
  3.1 4.5 %collective-permute-start = (f32[1,1,4,4,4,128]{5,4,3,2,1,0:T(4,128)S(1)}, f32[1,1,4,4,4,128]{5,4,3,2,1,0:T(4,128)S(1)}, u32[]{:S(2)}, u32[]{:S(2)}) collective-permute-start(f32[1,1,4,4,4,128]{5,4,3,2,1,0:T(4,128)S(1)} %bitcast.453), channel_id=1, source_target_pairs={{0,8},{8,16},{16,24},{1,9},{9,17},{17,25},{2,10},{10,18},{18,26},{... | collective-permute-start | bytes 98312 | tf_op jit(solution)/shard_map/ppermute | solution.py:18
  7.6 1.9 collective-permute-start.1
  10.4 2.5 collective-permute-done.1
  12.9 3.1 %collective-permute-start.2 = (f32[3,1,4,4,4,128]{5,4,3,2,1,0:T(4,128)S(1)}, f32[3,1,4,4,4,128]{5,4,3,2,1,0:T(4,128)S(1)}, u32[]{:S(2)}, u32[]{:S(2)}) collective-permute-start(f32[3,1,4,4,4,128]{5,4,3,2,1,0:T(4,128)S(1)} %pad_maximum_fusion), channel_id=1, source_target_pairs={{0,1},{1,2},{2,3},{3,4},{4,5},{5,6},{6,7},{8,9},{9,10},{10,11},{11... | collective-permute-start | bytes 294920 | tf_op jit(solution)/shard_map/ppermute | solution.py:18
  17.7 3.7 %collective-permute-done.3 = f32[3,1,4,4,4,128]{5,4,3,2,1,0:T(4,128)S(1)} collective-permute-done((f32[3,1,4,4,4,128]{5,4,3,2,1,0:T(4,128)S(1)}, f32[3,1,4,4,4,128]{5,4,3,2,1,0:T(4,128)S(1)}, u32[]{:S(2)}, u32[]{:S(2)}) %collective-permute-start.3) | collective-permute-done | bytes 98336 | tf_op jit(solution)/shard_map/ppermute | solution.py:19
  22.2 8.3 %constant_dynamic-update-slice_fusion.9 = (f32[24,4,128]{2,1,0:T(4,128)S(1)}, f32[8,4,128]{2,1,0:T(4,128)S(1)}) fusion(f32[8,14,4,128]{3,2,1,0:T(4,128)S(1)} %bitcast.438, f32[1,1,8,14,128,128]{5,4,3,2,1,0:T(8,128)} %param.16, f32[8,128]{1,0:T(8,128)} %bitcast.466, f32[1,1,8,4,128]{4,3,2,1,0:T(4,128)} %param.14), kind=kOutput, calls=%fused_computation.94 | convolution fusion | flops 88113152 | bytes 7622656 | tf_op jit(solution)/shard_map/bkij,bkrj->bri/dot_general | solution.py:35
  31.1 3.3 %collective-permute-start.4 = (f32[1,1,4,4,4,128]{5,4,3,2,1,0:T(4,128)S(1)}, f32[1,1,4,4,4,128]{5,4,3,2,1,0:T(4,128)S(1)}, u32[]{:S(2)}, u32[]{:S(2)}) collective-permute-start(f32[1,1,4,4,4,128]{5,4,3,2,1,0:T(4,128)S(1)} %bitcast.456), channel_id=1, source_target_pairs={{0,8},{8,16},{16,24},{1,9},{9,17},{17,25},{2,10},{10,18},{18,26},{... | collective-permute-start | bytes 98312 | tf_op jit(solution)/shard_map/ppermute | solution.py:18
  34.5 1.9 collective-permute-start.5
  36.5 3.2 %collective-permute-done.5 = f32[1,1,4,4,4,128]{5,4,3,2,1,0:T(4,128)S(1)} collective-permute-done((f32[1,1,4,4,4,128]{5,4,3,2,1,0:T(4,128)S(1)}, f32[1,1,4,4,4,128]{5,4,3,2,1,0:T(4,128)S(1)}, u32[]{:S(2)}, u32[]{:S(2)}) %collective-permute-start.5) | collective-permute-done | bytes 32800 | tf_op jit(solution)/shard_map/ppermute | solution.py:19
  39.7 4.0 %collective-permute-start.6 = (f32[3,1,4,4,4,128]{5,4,3,2,1,0:T(4,128)S(1)}, f32[3,1,4,4,4,128]{5,4,3,2,1,0:T(4,128)S(1)}, u32[]{:S(2)}, u32[]{:S(2)}) collective-permute-start(f32[3,1,4,4,4,128]{5,4,3,2,1,0:T(4,128)S(1)} %pad_maximum_fusion.1), channel_id=1, source_target_pairs={{0,1},{1,2},{2,3},{3,4},{4,5},{5,6},{6,7},{8,9},{9,10},{10,11},{11... | collective-permute-start | bytes 294920 | tf_op jit(solution)/shard_map/ppermute | solution.py:18
  45.4 3.7 %collective-permute-done.7 = f32[3,1,4,4,4,128]{5,4,3,2,1,0:T(4,128)S(1)} collective-permute-done((f32[3,1,4,4,4,128]{5,4,3,2,1,0:T(4,128)S(1)}, f32[3,1,4,4,4,128]{5,4,3,2,1,0:T(4,128)S(1)}, u32[]{:S(2)}, u32[]{:S(2)}) %collective-permute-start.7) | collective-permute-done | bytes 98336 | tf_op jit(solution)/shard_map/ppermute | solution.py:19
  49.9 8.2 %fusion.64 = f32[8,4,128]{2,1,0:T(4,128)S(1)} fusion(f32[8,14,4,128]{3,2,1,0:T(4,128)S(1)} %bitcast.440, f32[1,1,8,14,128,128]{5,4,3,2,1,0:T(8,128)} %param.16, f32[1,1,8,4,128]{4,3,2,1,0:T(4,128)S(1)} %copy-done.3, f32[8,4,128]{2,1,0:T(4,128)S(1)} %get-tuple-element.10, f32[8,128]{1,0:T(8,128)S(1)} %bitcast.467), kind=kOutput, calls=%fused_computation.50 | convolution fusion | flops 88092672 | bytes 7622656 | tf_op jit(solution)/shard_map/bkij,bkrj->bri/dot_general | solution.py:35
  59.4 3.3 %collective-permute-start.8 = (f32[1,1,4,2,4,128]{5,4,3,2,1,0:T(4,128)S(1)}, f32[1,1,4,2,4,128]{5,4,3,2,1,0:T(4,128)S(1)}, u32[]{:S(2)}, u32[]{:S(2)}) collective-permute-start(f32[1,1,4,2,4,128]{5,4,3,2,1,0:T(4,128)S(1)} %copy.90), channel_id=1, source_target_pairs={{0,8},{8,16},{16,24},{1,9},{9,17},{17,25},{2,10},{10,18},{18,26},{... | collective-permute-start | bytes 49160 | tf_op jit(solution)/shard_map/ppermute | solution.py:18
  62.8 1.9 collective-permute-start.9
  64.7 3.1 %collective-permute-done.9 = f32[1,1,4,2,4,128]{5,4,3,2,1,0:T(4,128)S(1)} collective-permute-done((f32[1,1,4,2,4,128]{5,4,3,2,1,0:T(4,128)S(1)}, f32[1,1,4,2,4,128]{5,4,3,2,1,0:T(4,128)S(1)}, u32[]{:S(2)}, u32[]{:S(2)}) %collective-permute-start.9) | collective-permute-done | bytes 16416 | tf_op jit(solution)/shard_map/ppermute | solution.py:19
  67.8 3.1 %collective-permute-start.10 = (f32[3,1,4,2,4,128]{5,4,3,2,1,0:T(4,128)S(1)}, f32[3,1,4,2,4,128]{5,4,3,2,1,0:T(4,128)S(1)}, u32[]{:S(2)}, u32[]{:S(2)}) collective-permute-start(f32[3,1,4,2,4,128]{5,4,3,2,1,0:T(4,128)S(1)} %constant_dynamic-update-slice_fusion.10), channel_id=1, source_target_pairs={{0,1},{1,2},{2,3},{3,4},{4,5},{5,6},{6,7},{8,9},{9,10},{10,11},{11... | collective-permute-start | bytes 147464 | tf_op jit(solution)/shard_map/ppermute | solution.py:18
  72.3 3.5 %collective-permute-done.11 = f32[3,1,4,2,4,128]{5,4,3,2,1,0:T(4,128)S(1)} collective-permute-done((f32[3,1,4,2,4,128]{5,4,3,2,1,0:T(4,128)S(1)}, f32[3,1,4,2,4,128]{5,4,3,2,1,0:T(4,128)S(1)}, u32[]{:S(2)}, u32[]{:S(2)}) %collective-permute-start.11) | collective-permute-done | bytes 49184 | tf_op jit(solution)/shard_map/ppermute | solution.py:19
  76.4 1.6 constant_dynamic-update-slice_fusion.25
  78.7 3.4 %collective-permute-start.12 = (f32[1,1,4,2,4,128]{5,4,3,2,1,0:T(4,128)S(1)}, f32[1,1,4,2,4,128]{5,4,3,2,1,0:T(4,128)S(1)}, u32[]{:S(2)}, u32[]{:S(2)}) collective-permute-start(f32[1,1,4,2,4,128]{5,4,3,2,1,0:T(4,128)S(1)} %copy.95), channel_id=1, source_target_pairs={{0,8},{8,16},{16,24},{1,9},{9,17},{17,25},{2,10},{10,18},{18,26},{... | collective-permute-start | bytes 49160 | tf_op jit(solution)/shard_map/ppermute | solution.py:18
  82.0 1.9 collective-permute-start.13
  84.0 3.1 %collective-permute-done.13 = f32[1,1,4,2,4,128]{5,4,3,2,1,0:T(4,128)S(1)} collective-permute-done((f32[1,1,4,2,4,128]{5,4,3,2,1,0:T(4,128)S(1)}, f32[1,1,4,2,4,128]{5,4,3,2,1,0:T(4,128)S(1)}, u32[]{:S(2)}, u32[]{:S(2)}) %collective-permute-start.13) | collective-permute-done | bytes 16416 | tf_op jit(solution)/shard_map/ppermute | solution.py:19
  87.1 4.0 %collective-permute-start.14 = (f32[3,1,4,2,4,128]{5,4,3,2,1,0:T(4,128)S(1)}, f32[3,1,4,2,4,128]{5,4,3,2,1,0:T(4,128)S(1)}, u32[]{:S(2)}, u32[]{:S(2)}) collective-permute-start(f32[3,1,4,2,4,128]{5,4,3,2,1,0:T(4,128)S(1)} %constant_dynamic-update-slice_fusion.18), channel_id=1, source_target_pairs={{0,1},{1,2},{2,3},{3,4},{4,5},{5,6},{6,7},{8,9},{9,10},{10,11},{11... | collective-permute-start | bytes 147464 | tf_op jit(solution)/shard_map/ppermute | solution.py:18
  92.5 3.5 %collective-permute-done.15 = f32[3,1,4,2,4,128]{5,4,3,2,1,0:T(4,128)S(1)} collective-permute-done((f32[3,1,4,2,4,128]{5,4,3,2,1,0:T(4,128)S(1)}, f32[3,1,4,2,4,128]{5,4,3,2,1,0:T(4,128)S(1)}, u32[]{:S(2)}, u32[]{:S(2)}) %collective-permute-start.15) | collective-permute-done | bytes 49184 | tf_op jit(solution)/shard_map/ppermute | solution.py:19
  98.7 39.2 %psum.7 = f32[4,1024]{1,0:T(4,128)S(1)} all-reduce(f32[4,1024]{1,0:T(4,128)S(1)} %bitcast.470), channel_id=1, replica_groups=mesh['row'=4,'col'=8] {'row','col'}, use_global_device_ids=true, to_apply=%region_0.0 | all-reduce | flops 4096 | bytes 32768 | tf_op jit(solution)/shard_map/psum | solution.py:79
  138.1 61.0 %all-gather = f32[32,32,4]{1,2,0:T(4,128)S(1)} all-gather(f32[1,32,4]{1,2,0:T(4,128)S(1)} %convolution_bitcast_fusion.1), channel_id=1, replica_groups=mesh['row'=4,'col'=8] {'row','col'}, dimensions={0}, use_global_device_ids=true | all-gather | bytes 16896 | tf_op jit(solution)/shard_map/all_gather | solution.py:81
  200.3 8.7 %collective-permute-start.16 = (f32[1,1,4,2,4,128]{5,4,3,2,1,0:T(4,128)S(1)}, f32[1,1,4,2,4,128]{5,4,3,2,1,0:T(4,128)S(1)}, u32[]{:S(2)}, u32[]{:S(2)}) collective-permute-start(f32[1,1,4,2,4,128]{5,4,3,2,1,0:T(4,128)S(1)} %copy.103), channel_id=1, source_target_pairs={{0,8},{8,16},{16,24},{1,9},{9,17},{17,25},{2,10},{10,18},{18,26},{... | collective-permute-start | bytes 49160 | tf_op jit(solution)/shard_map/ppermute | solution.py:18
  209.0 1.9 collective-permute-start.17
  211.0 3.1 %collective-permute-done.17 = f32[1,1,4,2,4,128]{5,4,3,2,1,0:T(4,128)S(1)} collective-permute-done((f32[1,1,4,2,4,128]{5,4,3,2,1,0:T(4,128)S(1)}, f32[1,1,4,2,4,128]{5,4,3,2,1,0:T(4,128)S(1)}, u32[]{:S(2)}, u32[]{:S(2)}) %collective-permute-start.17) | collective-permute-done | bytes 16416 | tf_op jit(solution)/shard_map/ppermute | solution.py:19
  214.1 3.4 %collective-permute-start.18 = (f32[3,1,4,2,4,128]{5,4,3,2,1,0:T(4,128)S(1)}, f32[3,1,4,2,4,128]{5,4,3,2,1,0:T(4,128)S(1)}, u32[]{:S(2)}, u32[]{:S(2)}) collective-permute-start(f32[3,1,4,2,4,128]{5,4,3,2,1,0:T(4,128)S(1)} %constant_dynamic-update-slice_fusion.26), channel_id=1, source_target_pairs={{0,1},{1,2},{2,3},{3,4},{4,5},{5,6},{6,7},{8,9},{9,10},{10,11},{11... | collective-permute-start | bytes 147464 | tf_op jit(solution)/shard_map/ppermute | solution.py:18
  218.8 3.5 %collective-permute-done.19 = f32[3,1,4,2,4,128]{5,4,3,2,1,0:T(4,128)S(1)} collective-permute-done((f32[3,1,4,2,4,128]{5,4,3,2,1,0:T(4,128)S(1)}, f32[3,1,4,2,4,128]{5,4,3,2,1,0:T(4,128)S(1)}, u32[]{:S(2)}, u32[]{:S(2)}) %collective-permute-start.19) | collective-permute-done | bytes 49184 | tf_op jit(solution)/shard_map/ppermute | solution.py:19
  222.9 1.6 constant_dynamic-update-slice_fusion.41
  225.1 3.4 %collective-permute-start.20 = (f32[1,1,4,2,4,128]{5,4,3,2,1,0:T(4,128)S(1)}, f32[1,1,4,2,4,128]{5,4,3,2,1,0:T(4,128)S(1)}, u32[]{:S(2)}, u32[]{:S(2)}) collective-permute-start(f32[1,1,4,2,4,128]{5,4,3,2,1,0:T(4,128)S(1)} %copy.108), channel_id=1, source_target_pairs={{0,8},{8,16},{16,24},{1,9},{9,17},{17,25},{2,10},{10,18},{18,26},{... | collective-permute-start | bytes 49160 | tf_op jit(solution)/shard_map/ppermute | solution.py:18
  228.5 1.9 collective-permute-start.21
  230.5 3.1 %collective-permute-done.21 = f32[1,1,4,2,4,128]{5,4,3,2,1,0:T(4,128)S(1)} collective-permute-done((f32[1,1,4,2,4,128]{5,4,3,2,1,0:T(4,128)S(1)}, f32[1,1,4,2,4,128]{5,4,3,2,1,0:T(4,128)S(1)}, u32[]{:S(2)}, u32[]{:S(2)}) %collective-permute-start.21) | collective-permute-done | bytes 16416 | tf_op jit(solution)/shard_map/ppermute | solution.py:19
  233.6 2.5 collective-permute-start.22
  237.4 3.5 %collective-permute-done.23 = f32[3,1,4,2,4,128]{5,4,3,2,1,0:T(4,128)S(1)} collective-permute-done((f32[3,1,4,2,4,128]{5,4,3,2,1,0:T(4,128)S(1)}, f32[3,1,4,2,4,128]{5,4,3,2,1,0:T(4,128)S(1)}, u32[]{:S(2)}, u32[]{:S(2)}) %collective-permute-start.23) | collective-permute-done | bytes 49184 | tf_op jit(solution)/shard_map/ppermute | solution.py:19
  244.9 3.4 %collective-permute-start.24 = (f32[1,1,4,4,4,128]{5,4,3,2,1,0:T(4,128)S(1)}, f32[1,1,4,4,4,128]{5,4,3,2,1,0:T(4,128)S(1)}, u32[]{:S(2)}, u32[]{:S(2)}) collective-permute-start(f32[1,1,4,4,4,128]{5,4,3,2,1,0:T(4,128)S(1)} %bitcast.462), channel_id=1, source_target_pairs={{0,8},{8,16},{16,24},{1,9},{9,17},{17,25},{2,10},{10,18},{18,26},{... | collective-permute-start | bytes 98312 | tf_op jit(solution)/shard_map/ppermute | solution.py:18
  248.3 1.9 collective-permute-start.25
  250.2 3.3 %collective-permute-done.25 = f32[1,1,4,4,4,128]{5,4,3,2,1,0:T(4,128)S(1)} collective-permute-done((f32[1,1,4,4,4,128]{5,4,3,2,1,0:T(4,128)S(1)}, f32[1,1,4,4,4,128]{5,4,3,2,1,0:T(4,128)S(1)}, u32[]{:S(2)}, u32[]{:S(2)}) %collective-permute-start.25) | collective-permute-done | bytes 32800 | tf_op jit(solution)/shard_map/ppermute | solution.py:19
  253.5 2.5 collective-permute-start.26
  257.7 3.7 %collective-permute-done.27 = f32[3,1,4,4,4,128]{5,4,3,2,1,0:T(4,128)S(1)} collective-permute-done((f32[3,1,4,4,4,128]{5,4,3,2,1,0:T(4,128)S(1)}, f32[3,1,4,4,4,128]{5,4,3,2,1,0:T(4,128)S(1)}, u32[]{:S(2)}, u32[]{:S(2)}) %collective-permute-start.27) | collective-permute-done | bytes 98336 | tf_op jit(solution)/shard_map/ppermute | solution.py:19
  262.2 8.2 %constant_dynamic-update-slice_fusion.51 = (f32[24,4,128]{2,1,0:T(4,128)S(1)}, f32[8,4,128]{2,1,0:T(4,128)S(1)}) fusion(f32[8,4,128]{2,1,0:T(4,128)S(1)} %get-tuple-element.18, f32[8,14,4,128]{3,2,1,0:T(4,128)S(1)} %bitcast.437, f32[1,1,8,14,128,128]{5,4,3,2,1,0:T(8,128)} %param.16, f32[8,128]{1,0:T(8,128)S(1)} %bitcast.468, ...), kind=kOutput, calls=%fused_computation.136 | convolution fusion | flops 88104960 | bytes 7639040 | tf_op jit(solution)/shard_map/bkij,bkrj->bri/dot_general | solution.py:35
  271.0 3.3 %collective-permute-start.28 = (f32[1,1,4,4,4,128]{5,4,3,2,1,0:T(4,128)S(1)}, f32[1,1,4,4,4,128]{5,4,3,2,1,0:T(4,128)S(1)}, u32[]{:S(2)}, u32[]{:S(2)}) collective-permute-start(f32[1,1,4,4,4,128]{5,4,3,2,1,0:T(4,128)S(1)} %bitcast.459), channel_id=1, source_target_pairs={{0,8},{8,16},{16,24},{1,9},{9,17},{17,25},{2,10},{10,18},{18,26},{... | collective-permute-start | bytes 98312 | tf_op jit(solution)/shard_map/ppermute | solution.py:18
  274.4 1.9 collective-permute-start.29
  276.3 3.3 %collective-permute-done.29 = f32[1,1,4,4,4,128]{5,4,3,2,1,0:T(4,128)S(1)} collective-permute-done((f32[1,1,4,4,4,128]{5,4,3,2,1,0:T(4,128)S(1)}, f32[1,1,4,4,4,128]{5,4,3,2,1,0:T(4,128)S(1)}, u32[]{:S(2)}, u32[]{:S(2)}) %collective-permute-start.29) | collective-permute-done | bytes 32800 | tf_op jit(solution)/shard_map/ppermute | solution.py:19
  279.6 2.5 collective-permute-start.30
  283.8 3.7 %collective-permute-done.31 = f32[3,1,4,4,4,128]{5,4,3,2,1,0:T(4,128)S(1)} collective-permute-done((f32[3,1,4,4,4,128]{5,4,3,2,1,0:T(4,128)S(1)}, f32[3,1,4,4,4,128]{5,4,3,2,1,0:T(4,128)S(1)}, u32[]{:S(2)}, u32[]{:S(2)}) %collective-permute-start.31) | collective-permute-done | bytes 98336 | tf_op jit(solution)/shard_map/ppermute | solution.py:19
  288.3 8.8 %fusion.43 = f32[1,1,8,4,128]{4,3,2,1,0:T(4,128)} fusion(f32[8,4,128]{2,1,0:T(4,128)S(1)} %get-tuple-element.20, f32[8,14,4,128]{3,2,1,0:T(4,128)S(1)} %bitcast.439, f32[1,1,8,14,128,128]{5,4,3,2,1,0:T(8,128)} %param.16, f32[1,1,8,4,128]{4,3,2,1,0:T(4,128)S(1)} %copy-done.3, f32[8,128]{1,0:T(8,128)S(1)} %bitcast.469), kind=kOutput, calls=%fused_computation.43 | convolution fusion | flops 88104960 | bytes 7622656 | tf_op jit(solution)/shard_map/bkij,bkrj->bri/dot_general | solution.py:35
  (144 shorter events, 31.8 us)
Async XLA Ops:
  0.0 76.4 %copy-start = (f32[1,1,2,14,128,128]{5,4,3,2,1,0:T(8,128)S(1)}, f32[1,1,2,14,128,128]{5,4,3,2,1,0:T(8,128)}, u32[]{:S(2)}) copy-start(f32[1,1,2,14,128,128]{5,4,3,2,1,0:T(8,128)} %param.22) | copy-start | bytes 5505028
  0.0 49.9 %copy-start.3 = (f32[1,1,8,4,128]{4,3,2,1,0:T(4,128)S(1)}, f32[1,1,8,4,128]{4,3,2,1,0:T(4,128)}, u32[]{:S(2)}) copy-start(f32[1,1,8,4,128]{4,3,2,1,0:T(4,128)} %param.14) | copy-start | bytes 49156
  0.0 49.9 %copy-start.5 = (f32[1,1,8,128]{3,2,1,0:T(8,128)S(1)}, f32[1,1,8,128]{3,2,1,0:T(8,128)}, u32[]{:S(2)}) copy-start(f32[1,1,8,128]{3,2,1,0:T(8,128)} %param.15) | copy-start | bytes 12292
  0.0 36.4 %copy-start.8 = (s32[1,1,2,14]{3,2,1,0:T(2,128)S(1)}, s32[1,1,2,14]{3,2,1,0:T(2,128)}, u32[]{:S(2)}) copy-start(s32[1,1,2,14]{3,2,1,0:T(2,128)} %param.23) | copy-start | bytes 340
  3.1 7.2 %collective-permute-start = (f32[1,1,4,4,4,128]{5,4,3,2,1,0:T(4,128)S(1)}, f32[1,1,4,4,4,128]{5,4,3,2,1,0:T(4,128)S(1)}, u32[]{:S(2)}, u32[]{:S(2)}) collective-permute-start(f32[1,1,4,4,4,128]{5,4,3,2,1,0:T(4,128)S(1)} %bitcast.453), channel_id=1, source_target_pairs={{0,8},{8,16},{16,24},{1,9},{9,17},{17,25},{2,10},{10,18},{18,26},{... | collective-permute-start | bytes 98312 | tf_op jit(solution)/shard_map/ppermute | solution.py:18
  7.6 5.2 %collective-permute-start.1 = (f32[1,1,4,4,4,128]{5,4,3,2,1,0:T(4,128)S(1)}, f32[1,1,4,4,4,128]{5,4,3,2,1,0:T(4,128)S(1)}, u32[]{:S(2)}, u32[]{:S(2)}) collective-permute-start(f32[1,1,4,4,4,128]{5,4,3,2,1,0:T(4,128)S(1)} %bitcast.454), channel_id=1, source_target_pairs={{8,0},{16,8},{24,16},{9,1},{17,9},{25,17},{10,2},{18,10},{26,18},{... | collective-permute-start | bytes 98312 | tf_op jit(solution)/shard_map/ppermute | solution.py:19
  12.9 4.8 %collective-permute-start.2 = (f32[3,1,4,4,4,128]{5,4,3,2,1,0:T(4,128)S(1)}, f32[3,1,4,4,4,128]{5,4,3,2,1,0:T(4,128)S(1)}, u32[]{:S(2)}, u32[]{:S(2)}) collective-permute-start(f32[3,1,4,4,4,128]{5,4,3,2,1,0:T(4,128)S(1)} %pad_maximum_fusion), channel_id=1, source_target_pairs={{0,1},{1,2},{2,3},{3,4},{4,5},{5,6},{6,7},{8,9},{9,10},{10,11},{11... | collective-permute-start | bytes 294920 | tf_op jit(solution)/shard_map/ppermute | solution.py:18
  16.1 5.4 %collective-permute-start.3 = (f32[3,1,4,4,4,128]{5,4,3,2,1,0:T(4,128)S(1)}, f32[3,1,4,4,4,128]{5,4,3,2,1,0:T(4,128)S(1)}, u32[]{:S(2)}, u32[]{:S(2)}) collective-permute-start(f32[3,1,4,4,4,128]{5,4,3,2,1,0:T(4,128)S(1)} %pad_maximum_fusion), channel_id=1, source_target_pairs={{1,0},{2,1},{3,2},{4,3},{5,4},{6,5},{7,6},{9,8},{10,9},{11,10},{12... | collective-permute-start | bytes 294920 | tf_op jit(solution)/shard_map/ppermute | solution.py:19
  22.2 36.0 %copy-start.1 = (f32[1,1,8,128,128]{4,3,2,1,0:T(8,128)S(1)}, f32[1,1,8,128,128]{4,3,2,1,0:T(8,128)}, u32[]{:S(2)}) copy-start(f32[1,1,8,128,128]{4,3,2,1,0:T(8,128)} %param.19) | copy-start | bytes 1572868
  22.2 36.5 %copy-start.7 = (s32[1,1,8]{2,1,0:T(1,128)S(1)}, s32[1,1,8]{2,1,0:T(1,128)}, u32[]{:S(2)}) copy-start(s32[1,1,8]{2,1,0:T(1,128)} %param.20) | copy-start | bytes 100
  22.2 36.6 %copy-start.6 = (f32[1,1,2,128]{3,2,1,0:T(2,128)S(1)}, f32[1,1,2,128]{3,2,1,0:T(2,128)}, u32[]{:S(2)}) copy-start(f32[1,1,2,128]{3,2,1,0:T(2,128)} %param.21) | copy-start | bytes 3076
  30.5 67.7 %copy-start.2 = (f32[1,1,2,128,128]{4,3,2,1,0:T(8,128)S(1)}, f32[1,1,2,128,128]{4,3,2,1,0:T(8,128)}, u32[]{:S(2)}) copy-start(f32[1,1,2,128,128]{4,3,2,1,0:T(8,128)} %param.25) | copy-start | bytes 393220
  30.5 67.9 %copy-start.9 = (s32[1,1,2]{2,1,0:T(1,128)S(1)}, s32[1,1,2]{2,1,0:T(1,128)}, u32[]{:S(2)}) copy-start(s32[1,1,2]{2,1,0:T(1,128)} %param.26) | copy-start | bytes 28
  30.5 107.4 %copy-start.4 = (f32[32,1024]{1,0:T(8,128)S(1)}, f32[32,1024]{1,0:T(8,128)}, u32[]{:S(2)}) copy-start(f32[32,1024]{1,0:T(8,128)} %param.27) | copy-start | bytes 393220
  31.1 5.4 %collective-permute-start.4 = (f32[1,1,4,4,4,128]{5,4,3,2,1,0:T(4,128)S(1)}, f32[1,1,4,4,4,128]{5,4,3,2,1,0:T(4,128)S(1)}, u32[]{:S(2)}, u32[]{:S(2)}) collective-permute-start(f32[1,1,4,4,4,128]{5,4,3,2,1,0:T(4,128)S(1)} %bitcast.456), channel_id=1, source_target_pairs={{0,8},{8,16},{16,24},{1,9},{9,17},{17,25},{2,10},{10,18},{18,26},{... | collective-permute-start | bytes 98312 | tf_op jit(solution)/shard_map/ppermute | solution.py:18
  34.5 5.2 %collective-permute-start.5 = (f32[1,1,4,4,4,128]{5,4,3,2,1,0:T(4,128)S(1)}, f32[1,1,4,4,4,128]{5,4,3,2,1,0:T(4,128)S(1)}, u32[]{:S(2)}, u32[]{:S(2)}) collective-permute-start(f32[1,1,4,4,4,128]{5,4,3,2,1,0:T(4,128)S(1)} %bitcast.457), channel_id=1, source_target_pairs={{8,0},{16,8},{24,16},{9,1},{17,9},{25,17},{10,2},{18,10},{26,18},{... | collective-permute-start | bytes 98312 | tf_op jit(solution)/shard_map/ppermute | solution.py:19
  39.7 5.7 %collective-permute-start.6 = (f32[3,1,4,4,4,128]{5,4,3,2,1,0:T(4,128)S(1)}, f32[3,1,4,4,4,128]{5,4,3,2,1,0:T(4,128)S(1)}, u32[]{:S(2)}, u32[]{:S(2)}) collective-permute-start(f32[3,1,4,4,4,128]{5,4,3,2,1,0:T(4,128)S(1)} %pad_maximum_fusion.1), channel_id=1, source_target_pairs={{0,1},{1,2},{2,3},{3,4},{4,5},{5,6},{6,7},{8,9},{9,10},{10,11},{11... | collective-permute-start | bytes 294920 | tf_op jit(solution)/shard_map/ppermute | solution.py:18
  43.8 5.4 %collective-permute-start.7 = (f32[3,1,4,4,4,128]{5,4,3,2,1,0:T(4,128)S(1)}, f32[3,1,4,4,4,128]{5,4,3,2,1,0:T(4,128)S(1)}, u32[]{:S(2)}, u32[]{:S(2)}) collective-permute-start(f32[3,1,4,4,4,128]{5,4,3,2,1,0:T(4,128)S(1)} %pad_maximum_fusion.1), channel_id=1, source_target_pairs={{1,0},{2,1},{3,2},{4,3},{5,4},{6,5},{7,6},{9,8},{10,9},{11,10},{12... | collective-permute-start | bytes 294920 | tf_op jit(solution)/shard_map/ppermute | solution.py:19
  59.4 5.3 %collective-permute-start.8 = (f32[1,1,4,2,4,128]{5,4,3,2,1,0:T(4,128)S(1)}, f32[1,1,4,2,4,128]{5,4,3,2,1,0:T(4,128)S(1)}, u32[]{:S(2)}, u32[]{:S(2)}) collective-permute-start(f32[1,1,4,2,4,128]{5,4,3,2,1,0:T(4,128)S(1)} %copy.90), channel_id=1, source_target_pairs={{0,8},{8,16},{16,24},{1,9},{9,17},{17,25},{2,10},{10,18},{18,26},{... | collective-permute-start | bytes 49160 | tf_op jit(solution)/shard_map/ppermute | solution.py:18
  62.8 5.1 %collective-permute-start.9 = (f32[1,1,4,2,4,128]{5,4,3,2,1,0:T(4,128)S(1)}, f32[1,1,4,2,4,128]{5,4,3,2,1,0:T(4,128)S(1)}, u32[]{:S(2)}, u32[]{:S(2)}) collective-permute-start(f32[1,1,4,2,4,128]{5,4,3,2,1,0:T(4,128)S(1)} %copy.90), channel_id=1, source_target_pairs={{8,0},{16,8},{24,16},{9,1},{17,9},{25,17},{10,2},{18,10},{26,18},{... | collective-permute-start | bytes 49160 | tf_op jit(solution)/shard_map/ppermute | solution.py:19
  67.8 4.5 %collective-permute-start.10 = (f32[3,1,4,2,4,128]{5,4,3,2,1,0:T(4,128)S(1)}, f32[3,1,4,2,4,128]{5,4,3,2,1,0:T(4,128)S(1)}, u32[]{:S(2)}, u32[]{:S(2)}) collective-permute-start(f32[3,1,4,2,4,128]{5,4,3,2,1,0:T(4,128)S(1)} %constant_dynamic-update-slice_fusion.10), channel_id=1, source_target_pairs={{0,1},{1,2},{2,3},{3,4},{4,5},{5,6},{6,7},{8,9},{9,10},{10,11},{11... | collective-permute-start | bytes 147464 | tf_op jit(solution)/shard_map/ppermute | solution.py:18
  71.0 4.8 %collective-permute-start.11 = (f32[3,1,4,2,4,128]{5,4,3,2,1,0:T(4,128)S(1)}, f32[3,1,4,2,4,128]{5,4,3,2,1,0:T(4,128)S(1)}, u32[]{:S(2)}, u32[]{:S(2)}) collective-permute-start(f32[3,1,4,2,4,128]{5,4,3,2,1,0:T(4,128)S(1)} %constant_dynamic-update-slice_fusion.10), channel_id=1, source_target_pairs={{1,0},{2,1},{3,2},{4,3},{5,4},{6,5},{7,6},{9,8},{10,9},{11,10},{12... | collective-permute-start | bytes 147464 | tf_op jit(solution)/shard_map/ppermute | solution.py:19
  78.7 5.3 %collective-permute-start.12 = (f32[1,1,4,2,4,128]{5,4,3,2,1,0:T(4,128)S(1)}, f32[1,1,4,2,4,128]{5,4,3,2,1,0:T(4,128)S(1)}, u32[]{:S(2)}, u32[]{:S(2)}) collective-permute-start(f32[1,1,4,2,4,128]{5,4,3,2,1,0:T(4,128)S(1)} %copy.95), channel_id=1, source_target_pairs={{0,8},{8,16},{16,24},{1,9},{9,17},{17,25},{2,10},{10,18},{18,26},{... | collective-permute-start | bytes 49160 | tf_op jit(solution)/shard_map/ppermute | solution.py:18
  82.0 5.1 %collective-permute-start.13 = (f32[1,1,4,2,4,128]{5,4,3,2,1,0:T(4,128)S(1)}, f32[1,1,4,2,4,128]{5,4,3,2,1,0:T(4,128)S(1)}, u32[]{:S(2)}, u32[]{:S(2)}) collective-permute-start(f32[1,1,4,2,4,128]{5,4,3,2,1,0:T(4,128)S(1)} %copy.95), channel_id=1, source_target_pairs={{8,0},{16,8},{24,16},{9,1},{17,9},{25,17},{10,2},{18,10},{26,18},{... | collective-permute-start | bytes 49160 | tf_op jit(solution)/shard_map/ppermute | solution.py:19
  87.1 5.4 %collective-permute-start.14 = (f32[3,1,4,2,4,128]{5,4,3,2,1,0:T(4,128)S(1)}, f32[3,1,4,2,4,128]{5,4,3,2,1,0:T(4,128)S(1)}, u32[]{:S(2)}, u32[]{:S(2)}) collective-permute-start(f32[3,1,4,2,4,128]{5,4,3,2,1,0:T(4,128)S(1)} %constant_dynamic-update-slice_fusion.18), channel_id=1, source_target_pairs={{0,1},{1,2},{2,3},{3,4},{4,5},{5,6},{6,7},{8,9},{9,10},{10,11},{11... | collective-permute-start | bytes 147464 | tf_op jit(solution)/shard_map/ppermute | solution.py:18
  91.1 4.8 %collective-permute-start.15 = (f32[3,1,4,2,4,128]{5,4,3,2,1,0:T(4,128)S(1)}, f32[3,1,4,2,4,128]{5,4,3,2,1,0:T(4,128)S(1)}, u32[]{:S(2)}, u32[]{:S(2)}) collective-permute-start(f32[3,1,4,2,4,128]{5,4,3,2,1,0:T(4,128)S(1)} %constant_dynamic-update-slice_fusion.18), channel_id=1, source_target_pairs={{1,0},{2,1},{3,2},{4,3},{5,4},{6,5},{7,6},{9,8},{10,9},{11,10},{12... | collective-permute-start | bytes 147464 | tf_op jit(solution)/shard_map/ppermute | solution.py:19
  200.3 10.6 %collective-permute-start.16 = (f32[1,1,4,2,4,128]{5,4,3,2,1,0:T(4,128)S(1)}, f32[1,1,4,2,4,128]{5,4,3,2,1,0:T(4,128)S(1)}, u32[]{:S(2)}, u32[]{:S(2)}) collective-permute-start(f32[1,1,4,2,4,128]{5,4,3,2,1,0:T(4,128)S(1)} %copy.103), channel_id=1, source_target_pairs={{0,8},{8,16},{16,24},{1,9},{9,17},{17,25},{2,10},{10,18},{18,26},{... | collective-permute-start | bytes 49160 | tf_op jit(solution)/shard_map/ppermute | solution.py:18
  209.0 5.1 %collective-permute-start.17 = (f32[1,1,4,2,4,128]{5,4,3,2,1,0:T(4,128)S(1)}, f32[1,1,4,2,4,128]{5,4,3,2,1,0:T(4,128)S(1)}, u32[]{:S(2)}, u32[]{:S(2)}) collective-permute-start(f32[1,1,4,2,4,128]{5,4,3,2,1,0:T(4,128)S(1)} %copy.103), channel_id=1, source_target_pairs={{8,0},{16,8},{24,16},{9,1},{17,9},{25,17},{10,2},{18,10},{26,18},{... | collective-permute-start | bytes 49160 | tf_op jit(solution)/shard_map/ppermute | solution.py:19
  214.1 4.7 %collective-permute-start.18 = (f32[3,1,4,2,4,128]{5,4,3,2,1,0:T(4,128)S(1)}, f32[3,1,4,2,4,128]{5,4,3,2,1,0:T(4,128)S(1)}, u32[]{:S(2)}, u32[]{:S(2)}) collective-permute-start(f32[3,1,4,2,4,128]{5,4,3,2,1,0:T(4,128)S(1)} %constant_dynamic-update-slice_fusion.26), channel_id=1, source_target_pairs={{0,1},{1,2},{2,3},{3,4},{4,5},{5,6},{6,7},{8,9},{9,10},{10,11},{11... | collective-permute-start | bytes 147464 | tf_op jit(solution)/shard_map/ppermute | solution.py:18
  217.5 4.8 %collective-permute-start.19 = (f32[3,1,4,2,4,128]{5,4,3,2,1,0:T(4,128)S(1)}, f32[3,1,4,2,4,128]{5,4,3,2,1,0:T(4,128)S(1)}, u32[]{:S(2)}, u32[]{:S(2)}) collective-permute-start(f32[3,1,4,2,4,128]{5,4,3,2,1,0:T(4,128)S(1)} %constant_dynamic-update-slice_fusion.26), channel_id=1, source_target_pairs={{1,0},{2,1},{3,2},{4,3},{5,4},{6,5},{7,6},{9,8},{10,9},{11,10},{12... | collective-permute-start | bytes 147464 | tf_op jit(solution)/shard_map/ppermute | solution.py:19
  225.1 5.3 %collective-permute-start.20 = (f32[1,1,4,2,4,128]{5,4,3,2,1,0:T(4,128)S(1)}, f32[1,1,4,2,4,128]{5,4,3,2,1,0:T(4,128)S(1)}, u32[]{:S(2)}, u32[]{:S(2)}) collective-permute-start(f32[1,1,4,2,4,128]{5,4,3,2,1,0:T(4,128)S(1)} %copy.108), channel_id=1, source_target_pairs={{0,8},{8,16},{16,24},{1,9},{9,17},{17,25},{2,10},{10,18},{18,26},{... | collective-permute-start | bytes 49160 | tf_op jit(solution)/shard_map/ppermute | solution.py:18
  228.5 5.1 %collective-permute-start.21 = (f32[1,1,4,2,4,128]{5,4,3,2,1,0:T(4,128)S(1)}, f32[1,1,4,2,4,128]{5,4,3,2,1,0:T(4,128)S(1)}, u32[]{:S(2)}, u32[]{:S(2)}) collective-permute-start(f32[1,1,4,2,4,128]{5,4,3,2,1,0:T(4,128)S(1)} %copy.108), channel_id=1, source_target_pairs={{8,0},{16,8},{24,16},{9,1},{17,9},{25,17},{10,2},{18,10},{26,18},{... | collective-permute-start | bytes 49160 | tf_op jit(solution)/shard_map/ppermute | solution.py:19
  233.6 3.9 %collective-permute-start.22 = (f32[3,1,4,2,4,128]{5,4,3,2,1,0:T(4,128)S(1)}, f32[3,1,4,2,4,128]{5,4,3,2,1,0:T(4,128)S(1)}, u32[]{:S(2)}, u32[]{:S(2)}) collective-permute-start(f32[3,1,4,2,4,128]{5,4,3,2,1,0:T(4,128)S(1)} %constant_dynamic-update-slice_fusion.34), channel_id=1, source_target_pairs={{0,1},{1,2},{2,3},{3,4},{4,5},{5,6},{6,7},{8,9},{9,10},{10,11},{11... | collective-permute-start | bytes 147464 | tf_op jit(solution)/shard_map/ppermute | solution.py:18
  236.1 4.8 %collective-permute-start.23 = (f32[3,1,4,2,4,128]{5,4,3,2,1,0:T(4,128)S(1)}, f32[3,1,4,2,4,128]{5,4,3,2,1,0:T(4,128)S(1)}, u32[]{:S(2)}, u32[]{:S(2)}) collective-permute-start(f32[3,1,4,2,4,128]{5,4,3,2,1,0:T(4,128)S(1)} %constant_dynamic-update-slice_fusion.34), channel_id=1, source_target_pairs={{1,0},{2,1},{3,2},{4,3},{5,4},{6,5},{7,6},{9,8},{10,9},{11,10},{12... | collective-permute-start | bytes 147464 | tf_op jit(solution)/shard_map/ppermute | solution.py:19
  244.9 5.3 %collective-permute-start.24 = (f32[1,1,4,4,4,128]{5,4,3,2,1,0:T(4,128)S(1)}, f32[1,1,4,4,4,128]{5,4,3,2,1,0:T(4,128)S(1)}, u32[]{:S(2)}, u32[]{:S(2)}) collective-permute-start(f32[1,1,4,4,4,128]{5,4,3,2,1,0:T(4,128)S(1)} %bitcast.462), channel_id=1, source_target_pairs={{0,8},{8,16},{16,24},{1,9},{9,17},{17,25},{2,10},{10,18},{18,26},{... | collective-permute-start | bytes 98312 | tf_op jit(solution)/shard_map/ppermute | solution.py:18
  248.3 5.2 %collective-permute-start.25 = (f32[1,1,4,4,4,128]{5,4,3,2,1,0:T(4,128)S(1)}, f32[1,1,4,4,4,128]{5,4,3,2,1,0:T(4,128)S(1)}, u32[]{:S(2)}, u32[]{:S(2)}) collective-permute-start(f32[1,1,4,4,4,128]{5,4,3,2,1,0:T(4,128)S(1)} %bitcast.463), channel_id=1, source_target_pairs={{8,0},{16,8},{24,16},{9,1},{17,9},{25,17},{10,2},{18,10},{26,18},{... | collective-permute-start | bytes 98312 | tf_op jit(solution)/shard_map/ppermute | solution.py:19
  253.5 4.2 %collective-permute-start.26 = (f32[3,1,4,4,4,128]{5,4,3,2,1,0:T(4,128)S(1)}, f32[3,1,4,4,4,128]{5,4,3,2,1,0:T(4,128)S(1)}, u32[]{:S(2)}, u32[]{:S(2)}) collective-permute-start(f32[3,1,4,4,4,128]{5,4,3,2,1,0:T(4,128)S(1)} %pad_maximum_fusion.2), channel_id=1, source_target_pairs={{0,1},{1,2},{2,3},{3,4},{4,5},{5,6},{6,7},{8,9},{9,10},{10,11},{11... | collective-permute-start | bytes 294920 | tf_op jit(solution)/shard_map/ppermute | solution.py:18
  256.1 5.4 %collective-permute-start.27 = (f32[3,1,4,4,4,128]{5,4,3,2,1,0:T(4,128)S(1)}, f32[3,1,4,4,4,128]{5,4,3,2,1,0:T(4,128)S(1)}, u32[]{:S(2)}, u32[]{:S(2)}) collective-permute-start(f32[3,1,4,4,4,128]{5,4,3,2,1,0:T(4,128)S(1)} %pad_maximum_fusion.2), channel_id=1, source_target_pairs={{1,0},{2,1},{3,2},{4,3},{5,4},{6,5},{7,6},{9,8},{10,9},{11,10},{12... | collective-permute-start | bytes 294920 | tf_op jit(solution)/shard_map/ppermute | solution.py:19
  271.0 5.3 %collective-permute-start.28 = (f32[1,1,4,4,4,128]{5,4,3,2,1,0:T(4,128)S(1)}, f32[1,1,4,4,4,128]{5,4,3,2,1,0:T(4,128)S(1)}, u32[]{:S(2)}, u32[]{:S(2)}) collective-permute-start(f32[1,1,4,4,4,128]{5,4,3,2,1,0:T(4,128)S(1)} %bitcast.459), channel_id=1, source_target_pairs={{0,8},{8,16},{16,24},{1,9},{9,17},{17,25},{2,10},{10,18},{18,26},{... | collective-permute-start | bytes 98312 | tf_op jit(solution)/shard_map/ppermute | solution.py:18
  274.4 5.2 %collective-permute-start.29 = (f32[1,1,4,4,4,128]{5,4,3,2,1,0:T(4,128)S(1)}, f32[1,1,4,4,4,128]{5,4,3,2,1,0:T(4,128)S(1)}, u32[]{:S(2)}, u32[]{:S(2)}) collective-permute-start(f32[1,1,4,4,4,128]{5,4,3,2,1,0:T(4,128)S(1)} %bitcast.460), channel_id=1, source_target_pairs={{8,0},{16,8},{24,16},{9,1},{17,9},{25,17},{10,2},{18,10},{26,18},{... | collective-permute-start | bytes 98312 | tf_op jit(solution)/shard_map/ppermute | solution.py:19
  279.6 4.2 %collective-permute-start.30 = (f32[3,1,4,4,4,128]{5,4,3,2,1,0:T(4,128)S(1)}, f32[3,1,4,4,4,128]{5,4,3,2,1,0:T(4,128)S(1)}, u32[]{:S(2)}, u32[]{:S(2)}) collective-permute-start(f32[3,1,4,4,4,128]{5,4,3,2,1,0:T(4,128)S(1)} %pad_maximum_fusion.3), channel_id=1, source_target_pairs={{0,1},{1,2},{2,3},{3,4},{4,5},{5,6},{6,7},{8,9},{9,10},{10,11},{11... | collective-permute-start | bytes 294920 | tf_op jit(solution)/shard_map/ppermute | solution.py:18
  282.2 5.4 %collective-permute-start.31 = (f32[3,1,4,4,4,128]{5,4,3,2,1,0:T(4,128)S(1)}, f32[3,1,4,4,4,128]{5,4,3,2,1,0:T(4,128)S(1)}, u32[]{:S(2)}, u32[]{:S(2)}) collective-permute-start(f32[3,1,4,4,4,128]{5,4,3,2,1,0:T(4,128)S(1)} %pad_maximum_fusion.3), channel_id=1, source_target_pairs={{1,0},{2,1},{3,2},{4,3},{5,4},{6,5},{7,6},{9,8},{10,9},{11,10},{12... | collective-permute-start | bytes 294920 | tf_op jit(solution)/shard_map/ppermute | solution.py:19
where the time goes:
time: 298 us; the launch traced here: 297 us
  blocking collectives  100 us (34%)
  starting transfers between devices  84.3 us (28%)
  waiting for transfers between devices  54.8 us (18%)
  matrix products  43 us (14%)
  local copies, waits for them, and re-layouts  11 us (4%)
  other arithmetic  3.06 us (1%)
    all_gather x1, blocking collectives, on_device(): coarse_x = lax.all_gather(own_rows, ('row', 'col'), axis=1, tiled=True)  61 us
    ppermute x16, starting transfers between devices, padded_2(): before = lax.ppermute(last, axis, up)  58.6 us
    ppermute x16, waiting for transfers between devices, padded_2(): after = lax.ppermute(leading, axis, down)  53.6 us
    dot_general x8, matrix products, apply_op(): coupled = jnp.einsum('bkij,bkrj->bri', blocks, nearby, precision=HIGH)  40 us
    psum x1, blocking collectives, on_device(): coarse_rhs = lax.psum(term, ('row', 'col'))  39.2 us
    ppermute x16, starting transfers between devices, padded_2(): after = lax.ppermute(leading, axis, down)  25.7 us
  transfers between devices with their start and end apart: 32, of which 20 were waited for; matrix products, arithmetic and copies ran while one was open for 0% of the time, Pallas kernels for 0%

commit v1 on v0

--- a/solution.py
+++ b/solution.py
@@ -76,7 +76,8 @@
     onehot1 = (agg1[0, 0][:, None] == jnp.arange(coarse_count)).astype(jnp.float32)
     contrib = jnp.einsum("bij,bri->brj", level_pro, level_res, precision=HIGH)
     term = jnp.einsum("bc,brj->rcj", onehot1, contrib, precision=HIGH).reshape(loads, coarse_total)
-    coarse_rhs = lax.psum(term, ("row", "col"))
+    parts = lax.all_gather(term, ("row", "col"), axis=0, tiled=False)
+    coarse_rhs = parts.sum(axis=0)
     own_rows = jnp.einsum("ij,rj->ri", cinv, coarse_rhs, precision=HIGH)
     coarse_x = lax.all_gather(own_rows, ("row", "col"), axis=1, tiled=True)
     coarse_blocks = coarse_x.reshape(loads, coarse_count, block_size)

time: 298 us -> 327 us (1.097); the launches traced: 297 us -> 321 us
  blocking collectives: 100 us -> 127 us
  waiting for transfers between devices: 54.8 us -> 31 us
  starting transfers between devices: 84.3 us -> 105 us
    all_gather x0 -> x1, blocking collectives: none -> 66.2 us  [on_device(): parts = lax.all_gather(term, ('row', 'col'), axis=0, tiled=False)]
    ppermute x16, waiting for transfers between devices: 53.6 us -> 12.4 us  [padded_2(): after = lax.ppermute(leading, axis, down)]
    psum x1 -> x0, blocking collectives: 39.2 us -> none  [on_device(): coarse_rhs = lax.psum(term, ('row', 'col'))]
    ppermute x16, starting transfers between devices: 58.6 us -> 78.9 us  [padded_2(): before = lax.ppermute(last, axis, up)]
    ppermute x16, waiting for transfers between devices: 1.2 us -> 18.6 us  [padded_2(): before = lax.ppermute(last, axis, up)]
  transfers between devices with their start and end apart: 32 -> 32, of which waited for: 20 -> 16; matrix products, arithmetic and copies ran while one was open for 0% -> 0% of each run, Pallas kernels for 0% -> 0%
where the time goes in v1:
time: 327 us; the launch traced here: 321 us
  blocking collectives  127 us (39%)
  starting transfers between devices  105 us (32%)
  matrix products  43 us (13%)
  waiting for transfers between devices  31 us (9%)
  local copies, waits for them, and re-layouts  11 us (3%)
    ppermute x16, starting transfers between devices, padded_2(): before = lax.ppermute(last, axis, up)  78.9 us
    all_gather x1, blocking collectives, on_device(): parts = lax.all_gather(term, ('row', 'col'), axis=0, tiled=False)  66.2 us
    all_gather x1, blocking collectives, on_device(): coarse_x = lax.all_gather(own_rows, ('row', 'col'), axis=1, tiled=True)  60.8 us
    dot_general x8, matrix products, apply_op(): coupled = jnp.einsum('bkij,bkrj->bri', blocks, nearby, precision=HIGH)  40 us
    ppermute x16, starting transfers between devices, padded_2(): after = lax.ppermute(leading, axis, down)  26.2 us
    ppermute x16, waiting for transfers between devices, padded_2(): before = lax.ppermute(last, axis, up)  18.6 us
    ppermute x16, waiting for transfers between devices, padded_2(): after = lax.ppermute(leading, axis, down)  12.4 us
  transfers between devices with their start and end apart: 32, of which 16 were waited for; matrix products, arithmetic and copies ran while one was open for 0% of the time, Pallas kernels for 0%

profile of v1, /device:TPU:1, one launch (start us, length us, event | category | flops | bytes accessed | tf_op | source)
XLA Modules:
  0.0 321.1 jit_solution(14593826248141654772)
XLA Ops:
  3.1 1.9 collective-permute-start.1
  5.1 4.5 %collective-permute-start = (f32[1,1,4,4,4,128]{5,4,3,2,1,0:T(4,128)S(1)}, f32[1,1,4,4,4,128]{5,4,3,2,1,0:T(4,128)S(1)}, u32[]{:S(2)}, u32[]{:S(2)}) collective-permute-start(f32[1,1,4,4,4,128]{5,4,3,2,1,0:T(4,128)S(1)} %bitcast.450), channel_id=1, source_target_pairs={{0,8},{8,16},{16,24},{1,9},{9,17},{17,25},{2,10},{10,18},{18,26},{... | collective-permute-start | bytes 98312 | tf_op jit(solution)/shard_map/ppermute | solution.py:18
  10.6 1.3 collective-permute-start.3
  11.9 4.0 %collective-permute-start.2 = (f32[3,1,4,4,4,128]{5,4,3,2,1,0:T(4,128)S(1)}, f32[3,1,4,4,4,128]{5,4,3,2,1,0:T(4,128)S(1)}, u32[]{:S(2)}, u32[]{:S(2)}) collective-permute-start(f32[3,1,4,4,4,128]{5,4,3,2,1,0:T(4,128)S(1)} %pad_maximum_fusion), channel_id=1, source_target_pairs={{0,1},{1,2},{2,3},{3,4},{4,5},{5,6},{6,7},{8,9},{9,10},{10,11},{11... | collective-permute-start | bytes 294920 | tf_op jit(solution)/shard_map/ppermute | solution.py:18
  15.9 3.2 collective-permute-done.2
  19.9 8.3 %constant_dynamic-update-slice_fusion.9 = (f32[24,4,128]{2,1,0:T(4,128)S(1)}, f32[8,4,128]{2,1,0:T(4,128)S(1)}) fusion(f32[8,14,4,128]{3,2,1,0:T(4,128)S(1)} %bitcast.434, f32[1,1,8,14,128,128]{5,4,3,2,1,0:T(8,128)} %param.16, f32[8,128]{1,0:T(8,128)} %bitcast.462, f32[1,1,8,4,128]{4,3,2,1,0:T(4,128)} %param.14), kind=kOutput, calls=%fused_computation.94 | convolution fusion | flops 88113152 | bytes 7622656 | tf_op jit(solution)/shard_map/bkij,bkrj->bri/dot_general | solution.py:35
  28.8 2.2 collective-permute-start.5
  31.0 3.5 %collective-permute-start.4 = (f32[1,1,4,4,4,128]{5,4,3,2,1,0:T(4,128)S(1)}, f32[1,1,4,4,4,128]{5,4,3,2,1,0:T(4,128)S(1)}, u32[]{:S(2)}, u32[]{:S(2)}) collective-permute-start(f32[1,1,4,4,4,128]{5,4,3,2,1,0:T(4,128)S(1)} %bitcast.453), channel_id=1, source_target_pairs={{0,8},{8,16},{16,24},{1,9},{9,17},{17,25},{2,10},{10,18},{18,26},{... | collective-permute-start | bytes 98312 | tf_op jit(solution)/shard_map/ppermute | solution.py:18
  35.5 1.4 collective-permute-start.7
  37.0 4.7 %collective-permute-start.6 = (f32[3,1,4,4,4,128]{5,4,3,2,1,0:T(4,128)S(1)}, f32[3,1,4,4,4,128]{5,4,3,2,1,0:T(4,128)S(1)}, u32[]{:S(2)}, u32[]{:S(2)}) collective-permute-start(f32[3,1,4,4,4,128]{5,4,3,2,1,0:T(4,128)S(1)} %pad_maximum_fusion.1), channel_id=1, source_target_pairs={{0,1},{1,2},{2,3},{3,4},{4,5},{5,6},{6,7},{8,9},{9,10},{10,11},{11... | collective-permute-start | bytes 294920 | tf_op jit(solution)/shard_map/ppermute | solution.py:18
  41.7 2.9 collective-permute-done.6
  45.4 8.2 %fusion.64 = f32[8,4,128]{2,1,0:T(4,128)S(1)} fusion(f32[8,14,4,128]{3,2,1,0:T(4,128)S(1)} %bitcast.436, f32[1,1,8,14,128,128]{5,4,3,2,1,0:T(8,128)} %param.16, f32[1,1,8,4,128]{4,3,2,1,0:T(4,128)S(1)} %copy-done.3, f32[8,4,128]{2,1,0:T(4,128)S(1)} %get-tuple-element.10, f32[8,128]{1,0:T(8,128)S(1)} %bitcast.463), kind=kOutput, calls=%fused_computation.50 | convolution fusion | flops 88092672 | bytes 7622656 | tf_op jit(solution)/shard_map/bkij,bkrj->bri/dot_general | solution.py:35
  54.9 4.1 %collective-permute-start.8 = (f32[1,1,4,2,4,128]{5,4,3,2,1,0:T(4,128)S(1)}, f32[1,1,4,2,4,128]{5,4,3,2,1,0:T(4,128)S(1)}, u32[]{:S(2)}, u32[]{:S(2)}) collective-permute-start(f32[1,1,4,2,4,128]{5,4,3,2,1,0:T(4,128)S(1)} %copy.90), channel_id=1, source_target_pairs={{0,8},{8,16},{16,24},{1,9},{9,17},{17,25},{2,10},{10,18},{18,26},{... | collective-permute-start | bytes 49160 | tf_op jit(solution)/shard_map/ppermute | solution.py:18
  59.0 1.9 collective-permute-start.9
  61.0 3.1 collective-permute-done.9
  64.1 1.3 collective-permute-start.11
  65.3 5.2 %collective-permute-start.10 = (f32[3,1,4,2,4,128]{5,4,3,2,1,0:T(4,128)S(1)}, f32[3,1,4,2,4,128]{5,4,3,2,1,0:T(4,128)S(1)}, u32[]{:S(2)}, u32[]{:S(2)}) collective-permute-start(f32[3,1,4,2,4,128]{5,4,3,2,1,0:T(4,128)S(1)} %constant_dynamic-update-slice_fusion.10), channel_id=1, source_target_pairs={{0,1},{1,2},{2,3},{3,4},{4,5},{5,6},{6,7},{8,9},{9,10},{10,11},{11... | collective-permute-start | bytes 147464 | tf_op jit(solution)/shard_map/ppermute | solution.py:18
  72.4 1.6 constant_dynamic-update-slice_fusion.25
  74.6 2.8 collective-permute-start.12
  77.4 1.9 collective-permute-start.13
  79.4 3.1 collective-permute-done.13
  82.5 1.3 collective-permute-start.15
  83.7 5.6 %collective-permute-start.14 = (f32[3,1,4,2,4,128]{5,4,3,2,1,0:T(4,128)S(1)}, f32[3,1,4,2,4,128]{5,4,3,2,1,0:T(4,128)S(1)}, u32[]{:S(2)}, u32[]{:S(2)}) collective-permute-start(f32[3,1,4,2,4,128]{5,4,3,2,1,0:T(4,128)S(1)} %constant_dynamic-update-slice_fusion.18), channel_id=1, source_target_pairs={{0,1},{1,2},{2,3},{3,4},{4,5},{5,6},{6,7},{8,9},{9,10},{10,11},{11... | collective-permute-start | bytes 147464 | tf_op jit(solution)/shard_map/ppermute | solution.py:18
  91.1 1.6 fusion.127
  93.2 66.2 %all_gather.6 = f32[32,4,1024]{2,1,0:T(4,128)S(1)} all-gather(f32[1,4,1024]{2,1,0:T(4,128)S(1)} %all_gather_reshape.3), channel_id=1, replica_groups=mesh['row'=4,'col'=8] {'row','col'}, dimensions={0}, use_global_device_ids=true | all-gather | bytes 540672 | tf_op jit(solution)/shard_map/all_gather | solution.py:79
  159.7 60.8 %all-gather = f32[32,32,4]{1,2,0:T(4,128)S(1)} all-gather(f32[1,32,4]{1,2,0:T(4,128)S(1)} %convolution_bitcast_fusion.1), channel_id=1, replica_groups=mesh['row'=4,'col'=8] {'row','col'}, dimensions={0}, use_global_device_ids=true | all-gather | bytes 16896 | tf_op jit(solution)/shard_map/all_gather | solution.py:82
  221.8 14.0 %collective-permute-start.16 = (f32[1,1,4,2,4,128]{5,4,3,2,1,0:T(4,128)S(1)}, f32[1,1,4,2,4,128]{5,4,3,2,1,0:T(4,128)S(1)}, u32[]{:S(2)}, u32[]{:S(2)}) collective-permute-start(f32[1,1,4,2,4,128]{5,4,3,2,1,0:T(4,128)S(1)} %copy.103), channel_id=1, source_target_pairs={{0,8},{8,16},{16,24},{1,9},{9,17},{17,25},{2,10},{10,18},{18,26},{... | collective-permute-start | bytes 49160 | tf_op jit(solution)/shard_map/ppermute | solution.py:18
  235.7 1.9 collective-permute-start.17
  237.7 3.1 collective-permute-done.17
  242.1 4.7 %collective-permute-start.18 = (f32[3,1,4,2,4,128]{5,4,3,2,1,0:T(4,128)S(1)}, f32[3,1,4,2,4,128]{5,4,3,2,1,0:T(4,128)S(1)}, u32[]{:S(2)}, u32[]{:S(2)}) collective-permute-start(f32[3,1,4,2,4,128]{5,4,3,2,1,0:T(4,128)S(1)} %constant_dynamic-update-slice_fusion.26), channel_id=1, source_target_pairs={{0,1},{1,2},{2,3},{3,4},{4,5},{5,6},{6,7},{8,9},{9,10},{10,11},{11... | collective-permute-start | bytes 147464 | tf_op jit(solution)/shard_map/ppermute | solution.py:18
  248.4 1.6 constant_dynamic-update-slice_fusion.41
  250.6 2.8 collective-permute-start.20
  253.4 1.9 collective-permute-start.21
  255.4 3.1 collective-permute-done.21
  259.8 5.2 %collective-permute-start.22 = (f32[3,1,4,2,4,128]{5,4,3,2,1,0:T(4,128)S(1)}, f32[3,1,4,2,4,128]{5,4,3,2,1,0:T(4,128)S(1)}, u32[]{:S(2)}, u32[]{:S(2)}) collective-permute-start(f32[3,1,4,2,4,128]{5,4,3,2,1,0:T(4,128)S(1)} %constant_dynamic-update-slice_fusion.34), channel_id=1, source_target_pairs={{0,1},{1,2},{2,3},{3,4},{4,5},{5,6},{6,7},{8,9},{9,10},{10,11},{11... | collective-permute-start | bytes 147464 | tf_op jit(solution)/shard_map/ppermute | solution.py:18
  266.7 1.6 fusion.106
  270.1 1.9 collective-permute-start.25
  272.0 3.6 %collective-permute-start.24 = (f32[1,1,4,4,4,128]{5,4,3,2,1,0:T(4,128)S(1)}, f32[1,1,4,4,4,128]{5,4,3,2,1,0:T(4,128)S(1)}, u32[]{:S(2)}, u32[]{:S(2)}) collective-permute-start(f32[1,1,4,4,4,128]{5,4,3,2,1,0:T(4,128)S(1)} %bitcast.459), channel_id=1, source_target_pairs={{0,8},{8,16},{16,24},{1,9},{9,17},{17,25},{2,10},{10,18},{18,26},{... | collective-permute-start | bytes 98312 | tf_op jit(solution)/shard_map/ppermute | solution.py:18
  276.7 1.3 collective-permute-start.27
  278.0 5.5 %collective-permute-start.26 = (f32[3,1,4,4,4,128]{5,4,3,2,1,0:T(4,128)S(1)}, f32[3,1,4,4,4,128]{5,4,3,2,1,0:T(4,128)S(1)}, u32[]{:S(2)}, u32[]{:S(2)}) collective-permute-start(f32[3,1,4,4,4,128]{5,4,3,2,1,0:T(4,128)S(1)} %pad_maximum_fusion.2), channel_id=1, source_target_pairs={{0,1},{1,2},{2,3},{3,4},{4,5},{5,6},{6,7},{8,9},{9,10},{10,11},{11... | collective-permute-start | bytes 294920 | tf_op jit(solution)/shard_map/ppermute | solution.py:18
  283.5 2.8 collective-permute-done.26
  287.1 8.2 %constant_dynamic-update-slice_fusion.51 = (f32[24,4,128]{2,1,0:T(4,128)S(1)}, f32[8,4,128]{2,1,0:T(4,128)S(1)}) fusion(f32[8,4,128]{2,1,0:T(4,128)S(1)} %get-tuple-element.18, f32[8,14,4,128]{3,2,1,0:T(4,128)S(1)} %bitcast.433, f32[1,1,8,14,128,128]{5,4,3,2,1,0:T(8,128)} %param.16, f32[8,128]{1,0:T(8,128)S(1)} %bitcast.464, ...), kind=kOutput, calls=%fused_computation.136 | convolution fusion | flops 88104960 | bytes 7639040 | tf_op jit(solution)/shard_map/bkij,bkrj->bri/dot_general | solution.py:35
  295.9 2.1 collective-permute-start.29
  298.0 3.7 %collective-permute-start.28 = (f32[1,1,4,4,4,128]{5,4,3,2,1,0:T(4,128)S(1)}, f32[1,1,4,4,4,128]{5,4,3,2,1,0:T(4,128)S(1)}, u32[]{:S(2)}, u32[]{:S(2)}) collective-permute-start(f32[1,1,4,4,4,128]{5,4,3,2,1,0:T(4,128)S(1)} %bitcast.456), channel_id=1, source_target_pairs={{0,8},{8,16},{16,24},{1,9},{9,17},{17,25},{2,10},{10,18},{18,26},{... | collective-permute-start | bytes 98312 | tf_op jit(solution)/shard_map/ppermute | solution.py:18
  302.7 1.3 collective-permute-start.31
  304.0 5.2 %collective-permute-start.30 = (f32[3,1,4,4,4,128]{5,4,3,2,1,0:T(4,128)S(1)}, f32[3,1,4,4,4,128]{5,4,3,2,1,0:T(4,128)S(1)}, u32[]{:S(2)}, u32[]{:S(2)}) collective-permute-start(f32[3,1,4,4,4,128]{5,4,3,2,1,0:T(4,128)S(1)} %pad_maximum_fusion.3), channel_id=1, source_target_pairs={{0,1},{1,2},{2,3},{3,4},{4,5},{5,6},{6,7},{8,9},{9,10},{10,11},{11... | collective-permute-start | bytes 294920 | tf_op jit(solution)/shard_map/ppermute | solution.py:18
  309.3 2.2 collective-permute-done.30
  312.2 8.8 %fusion.43 = f32[1,1,8,4,128]{4,3,2,1,0:T(4,128)} fusion(f32[8,4,128]{2,1,0:T(4,128)S(1)} %get-tuple-element.20, f32[8,14,4,128]{3,2,1,0:T(4,128)S(1)} %bitcast.435, f32[1,1,8,14,128,128]{5,4,3,2,1,0:T(8,128)} %param.16, f32[1,1,8,4,128]{4,3,2,1,0:T(4,128)S(1)} %copy-done.3, f32[8,128]{1,0:T(8,128)S(1)} %bitcast.465), kind=kOutput, calls=%fused_computation.43 | convolution fusion | flops 88104960 | bytes 7622656 | tf_op jit(solution)/shard_map/bkij,bkrj->bri/dot_general | solution.py:35
  (145 shorter events, 27.2 us)
Async XLA Ops:
  0.0 72.4 %copy-start = (f32[1,1,2,14,128,128]{5,4,3,2,1,0:T(8,128)S(1)}, f32[1,1,2,14,128,128]{5,4,3,2,1,0:T(8,128)}, u32[]{:S(2)}) copy-start(f32[1,1,2,14,128,128]{5,4,3,2,1,0:T(8,128)} %param.22) | copy-start | bytes 5505028
  0.0 45.3 %copy-start.3 = (f32[1,1,8,4,128]{4,3,2,1,0:T(4,128)S(1)}, f32[1,1,8,4,128]{4,3,2,1,0:T(4,128)}, u32[]{:S(2)}) copy-start(f32[1,1,8,4,128]{4,3,2,1,0:T(4,128)} %param.14) | copy-start | bytes 49156
  0.0 45.4 %copy-start.5 = (f32[1,1,8,128]{3,2,1,0:T(8,128)S(1)}, f32[1,1,8,128]{3,2,1,0:T(8,128)}, u32[]{:S(2)}) copy-start(f32[1,1,8,128]{3,2,1,0:T(8,128)} %param.15) | copy-start | bytes 12292
  0.0 34.5 %copy-start.8 = (s32[1,1,2,14]{3,2,1,0:T(2,128)S(1)}, s32[1,1,2,14]{3,2,1,0:T(2,128)}, u32[]{:S(2)}) copy-start(s32[1,1,2,14]{3,2,1,0:T(2,128)} %param.23) | copy-start | bytes 340
  3.1 7.2 %collective-permute-start.1 = (f32[1,1,4,4,4,128]{5,4,3,2,1,0:T(4,128)S(1)}, f32[1,1,4,4,4,128]{5,4,3,2,1,0:T(4,128)S(1)}, u32[]{:S(2)}, u32[]{:S(2)}) collective-permute-start(f32[1,1,4,4,4,128]{5,4,3,2,1,0:T(4,128)S(1)} %bitcast.449), channel_id=1, source_target_pairs={{8,0},{16,8},{24,16},{9,1},{17,9},{25,17},{10,2},{18,10},{26,18},{... | collective-permute-start | bytes 98312 | tf_op jit(solution)/shard_map/ppermute | solution.py:19
  5.1 5.5 %collective-permute-start = (f32[1,1,4,4,4,128]{5,4,3,2,1,0:T(4,128)S(1)}, f32[1,1,4,4,4,128]{5,4,3,2,1,0:T(4,128)S(1)}, u32[]{:S(2)}, u32[]{:S(2)}) collective-permute-start(f32[1,1,4,4,4,128]{5,4,3,2,1,0:T(4,128)S(1)} %bitcast.450), channel_id=1, source_target_pairs={{0,8},{8,16},{16,24},{1,9},{9,17},{17,25},{2,10},{10,18},{18,26},{... | collective-permute-start | bytes 98312 | tf_op jit(solution)/shard_map/ppermute | solution.py:18
  10.6 8.5 %collective-permute-start.3 = (f32[3,1,4,4,4,128]{5,4,3,2,1,0:T(4,128)S(1)}, f32[3,1,4,4,4,128]{5,4,3,2,1,0:T(4,128)S(1)}, u32[]{:S(2)}, u32[]{:S(2)}) collective-permute-start(f32[3,1,4,4,4,128]{5,4,3,2,1,0:T(4,128)S(1)} %pad_maximum_fusion), channel_id=1, source_target_pairs={{1,0},{2,1},{3,2},{4,3},{5,4},{6,5},{7,6},{9,8},{10,9},{11,10},{12... | collective-permute-start | bytes 294920 | tf_op jit(solution)/shard_map/ppermute | solution.py:19
  11.9 7.2 %collective-permute-start.2 = (f32[3,1,4,4,4,128]{5,4,3,2,1,0:T(4,128)S(1)}, f32[3,1,4,4,4,128]{5,4,3,2,1,0:T(4,128)S(1)}, u32[]{:S(2)}, u32[]{:S(2)}) collective-permute-start(f32[3,1,4,4,4,128]{5,4,3,2,1,0:T(4,128)S(1)} %pad_maximum_fusion), channel_id=1, source_target_pairs={{0,1},{1,2},{2,3},{3,4},{4,5},{5,6},{6,7},{8,9},{9,10},{10,11},{11... | collective-permute-start | bytes 294920 | tf_op jit(solution)/shard_map/ppermute | solution.py:18
  19.8 33.8 %copy-start.1 = (f32[1,1,8,128,128]{4,3,2,1,0:T(8,128)S(1)}, f32[1,1,8,128,128]{4,3,2,1,0:T(8,128)}, u32[]{:S(2)}) copy-start(f32[1,1,8,128,128]{4,3,2,1,0:T(8,128)} %param.19) | copy-start | bytes 1572868
  19.8 34.3 %copy-start.7 = (s32[1,1,8]{2,1,0:T(1,128)S(1)}, s32[1,1,8]{2,1,0:T(1,128)}, u32[]{:S(2)}) copy-start(s32[1,1,8]{2,1,0:T(1,128)} %param.20) | copy-start | bytes 100
  19.9 34.4 %copy-start.6 = (f32[1,1,2,128]{3,2,1,0:T(2,128)S(1)}, f32[1,1,2,128]{3,2,1,0:T(2,128)}, u32[]{:S(2)}) copy-start(f32[1,1,2,128]{3,2,1,0:T(2,128)} %param.21) | copy-start | bytes 3076
  28.2 64.5 %copy-start.2 = (f32[1,1,2,128,128]{4,3,2,1,0:T(8,128)S(1)}, f32[1,1,2,128,128]{4,3,2,1,0:T(8,128)}, u32[]{:S(2)}) copy-start(f32[1,1,2,128,128]{4,3,2,1,0:T(8,128)} %param.25) | copy-start | bytes 393220
  28.2 64.8 %copy-start.9 = (s32[1,1,2]{2,1,0:T(1,128)S(1)}, s32[1,1,2]{2,1,0:T(1,128)}, u32[]{:S(2)}) copy-start(s32[1,1,2]{2,1,0:T(1,128)} %param.26) | copy-start | bytes 28
  28.8 5.8 %collective-permute-start.5 = (f32[1,1,4,4,4,128]{5,4,3,2,1,0:T(4,128)S(1)}, f32[1,1,4,4,4,128]{5,4,3,2,1,0:T(4,128)S(1)}, u32[]{:S(2)}, u32[]{:S(2)}) collective-permute-start(f32[1,1,4,4,4,128]{5,4,3,2,1,0:T(4,128)S(1)} %bitcast.452), channel_id=1, source_target_pairs={{8,0},{16,8},{24,16},{9,1},{17,9},{25,17},{10,2},{18,10},{26,18},{... | collective-permute-start | bytes 98312 | tf_op jit(solution)/shard_map/ppermute | solution.py:19
  31.0 4.5 %collective-permute-start.4 = (f32[1,1,4,4,4,128]{5,4,3,2,1,0:T(4,128)S(1)}, f32[1,1,4,4,4,128]{5,4,3,2,1,0:T(4,128)S(1)}, u32[]{:S(2)}, u32[]{:S(2)}) collective-permute-start(f32[1,1,4,4,4,128]{5,4,3,2,1,0:T(4,128)S(1)} %bitcast.453), channel_id=1, source_target_pairs={{0,8},{8,16},{16,24},{1,9},{9,17},{17,25},{2,10},{10,18},{18,26},{... | collective-permute-start | bytes 98312 | tf_op jit(solution)/shard_map/ppermute | solution.py:18
  35.5 124.0 %copy-start.4 = (f32[32,1024]{1,0:T(8,128)S(1)}, f32[32,1024]{1,0:T(8,128)}, u32[]{:S(2)}) copy-start(f32[32,1024]{1,0:T(8,128)} %param.27) | copy-start | bytes 393220
  35.5 9.1 %collective-permute-start.7 = (f32[3,1,4,4,4,128]{5,4,3,2,1,0:T(4,128)S(1)}, f32[3,1,4,4,4,128]{5,4,3,2,1,0:T(4,128)S(1)}, u32[]{:S(2)}, u32[]{:S(2)}) collective-permute-start(f32[3,1,4,4,4,128]{5,4,3,2,1,0:T(4,128)S(1)} %pad_maximum_fusion.1), channel_id=1, source_target_pairs={{1,0},{2,1},{3,2},{4,3},{5,4},{6,5},{7,6},{9,8},{10,9},{11,10},{12... | collective-permute-start | bytes 294920 | tf_op jit(solution)/shard_map/ppermute | solution.py:19
  37.0 7.6 %collective-permute-start.6 = (f32[3,1,4,4,4,128]{5,4,3,2,1,0:T(4,128)S(1)}, f32[3,1,4,4,4,128]{5,4,3,2,1,0:T(4,128)S(1)}, u32[]{:S(2)}, u32[]{:S(2)}) collective-permute-start(f32[3,1,4,4,4,128]{5,4,3,2,1,0:T(4,128)S(1)} %pad_maximum_fusion.1), channel_id=1, source_target_pairs={{0,1},{1,2},{2,3},{3,4},{4,5},{5,6},{6,7},{8,9},{9,10},{10,11},{11... | collective-permute-start | bytes 294920 | tf_op jit(solution)/shard_map/ppermute | solution.py:18
  54.9 6.0 %collective-permute-start.8 = (f32[1,1,4,2,4,128]{5,4,3,2,1,0:T(4,128)S(1)}, f32[1,1,4,2,4,128]{5,4,3,2,1,0:T(4,128)S(1)}, u32[]{:S(2)}, u32[]{:S(2)}) collective-permute-start(f32[1,1,4,2,4,128]{5,4,3,2,1,0:T(4,128)S(1)} %copy.90), channel_id=1, source_target_pairs={{0,8},{8,16},{16,24},{1,9},{9,17},{17,25},{2,10},{10,18},{18,26},{... | collective-permute-start | bytes 49160 | tf_op jit(solution)/shard_map/ppermute | solution.py:18
  59.0 5.1 %collective-permute-start.9 = (f32[1,1,4,2,4,128]{5,4,3,2,1,0:T(4,128)S(1)}, f32[1,1,4,2,4,128]{5,4,3,2,1,0:T(4,128)S(1)}, u32[]{:S(2)}, u32[]{:S(2)}) collective-permute-start(f32[1,1,4,2,4,128]{5,4,3,2,1,0:T(4,128)S(1)} %copy.90), channel_id=1, source_target_pairs={{8,0},{16,8},{24,16},{9,1},{17,9},{25,17},{10,2},{18,10},{26,18},{... | collective-permute-start | bytes 49160 | tf_op jit(solution)/shard_map/ppermute | solution.py:19
  64.1 7.7 %collective-permute-start.11 = (f32[3,1,4,2,4,128]{5,4,3,2,1,0:T(4,128)S(1)}, f32[3,1,4,2,4,128]{5,4,3,2,1,0:T(4,128)S(1)}, u32[]{:S(2)}, u32[]{:S(2)}) collective-permute-start(f32[3,1,4,2,4,128]{5,4,3,2,1,0:T(4,128)S(1)} %constant_dynamic-update-slice_fusion.10), channel_id=1, source_target_pairs={{1,0},{2,1},{3,2},{4,3},{5,4},{6,5},{7,6},{9,8},{10,9},{11,10},{12... | collective-permute-start | bytes 147464 | tf_op jit(solution)/shard_map/ppermute | solution.py:19
  65.3 6.4 %collective-permute-start.10 = (f32[3,1,4,2,4,128]{5,4,3,2,1,0:T(4,128)S(1)}, f32[3,1,4,2,4,128]{5,4,3,2,1,0:T(4,128)S(1)}, u32[]{:S(2)}, u32[]{:S(2)}) collective-permute-start(f32[3,1,4,2,4,128]{5,4,3,2,1,0:T(4,128)S(1)} %constant_dynamic-update-slice_fusion.10), channel_id=1, source_target_pairs={{0,1},{1,2},{2,3},{3,4},{4,5},{5,6},{6,7},{8,9},{9,10},{10,11},{11... | collective-permute-start | bytes 147464 | tf_op jit(solution)/shard_map/ppermute | solution.py:18
  74.6 4.7 %collective-permute-start.12 = (f32[1,1,4,2,4,128]{5,4,3,2,1,0:T(4,128)S(1)}, f32[1,1,4,2,4,128]{5,4,3,2,1,0:T(4,128)S(1)}, u32[]{:S(2)}, u32[]{:S(2)}) collective-permute-start(f32[1,1,4,2,4,128]{5,4,3,2,1,0:T(4,128)S(1)} %copy.95), channel_id=1, source_target_pairs={{0,8},{8,16},{16,24},{1,9},{9,17},{17,25},{2,10},{10,18},{18,26},{... | collective-permute-start | bytes 49160 | tf_op jit(solution)/shard_map/ppermute | solution.py:18
  77.4 5.1 %collective-permute-start.13 = (f32[1,1,4,2,4,128]{5,4,3,2,1,0:T(4,128)S(1)}, f32[1,1,4,2,4,128]{5,4,3,2,1,0:T(4,128)S(1)}, u32[]{:S(2)}, u32[]{:S(2)}) collective-permute-start(f32[1,1,4,2,4,128]{5,4,3,2,1,0:T(4,128)S(1)} %copy.95), channel_id=1, source_target_pairs={{8,0},{16,8},{24,16},{9,1},{17,9},{25,17},{10,2},{18,10},{26,18},{... | collective-permute-start | bytes 49160 | tf_op jit(solution)/shard_map/ppermute | solution.py:19
  82.5 8.0 %collective-permute-start.15 = (f32[3,1,4,2,4,128]{5,4,3,2,1,0:T(4,128)S(1)}, f32[3,1,4,2,4,128]{5,4,3,2,1,0:T(4,128)S(1)}, u32[]{:S(2)}, u32[]{:S(2)}) collective-permute-start(f32[3,1,4,2,4,128]{5,4,3,2,1,0:T(4,128)S(1)} %constant_dynamic-update-slice_fusion.18), channel_id=1, source_target_pairs={{1,0},{2,1},{3,2},{4,3},{5,4},{6,5},{7,6},{9,8},{10,9},{11,10},{12... | collective-permute-start | bytes 147464 | tf_op jit(solution)/shard_map/ppermute | solution.py:19
  83.7 6.7 %collective-permute-start.14 = (f32[3,1,4,2,4,128]{5,4,3,2,1,0:T(4,128)S(1)}, f32[3,1,4,2,4,128]{5,4,3,2,1,0:T(4,128)S(1)}, u32[]{:S(2)}, u32[]{:S(2)}) collective-permute-start(f32[3,1,4,2,4,128]{5,4,3,2,1,0:T(4,128)S(1)} %constant_dynamic-update-slice_fusion.18), channel_id=1, source_target_pairs={{0,1},{1,2},{2,3},{3,4},{4,5},{5,6},{6,7},{8,9},{9,10},{10,11},{11... | collective-permute-start | bytes 147464 | tf_op jit(solution)/shard_map/ppermute | solution.py:18
  221.8 15.9 %collective-permute-start.16 = (f32[1,1,4,2,4,128]{5,4,3,2,1,0:T(4,128)S(1)}, f32[1,1,4,2,4,128]{5,4,3,2,1,0:T(4,128)S(1)}, u32[]{:S(2)}, u32[]{:S(2)}) collective-permute-start(f32[1,1,4,2,4,128]{5,4,3,2,1,0:T(4,128)S(1)} %copy.103), channel_id=1, source_target_pairs={{0,8},{8,16},{16,24},{1,9},{9,17},{17,25},{2,10},{10,18},{18,26},{... | collective-permute-start | bytes 49160 | tf_op jit(solution)/shard_map/ppermute | solution.py:18
  235.7 5.1 %collective-permute-start.17 = (f32[1,1,4,2,4,128]{5,4,3,2,1,0:T(4,128)S(1)}, f32[1,1,4,2,4,128]{5,4,3,2,1,0:T(4,128)S(1)}, u32[]{:S(2)}, u32[]{:S(2)}) collective-permute-start(f32[1,1,4,2,4,128]{5,4,3,2,1,0:T(4,128)S(1)} %copy.103), channel_id=1, source_target_pairs={{8,0},{16,8},{24,16},{9,1},{17,9},{25,17},{10,2},{18,10},{26,18},{... | collective-permute-start | bytes 49160 | tf_op jit(solution)/shard_map/ppermute | solution.py:19
  240.8 7.0 %collective-permute-start.19 = (f32[3,1,4,2,4,128]{5,4,3,2,1,0:T(4,128)S(1)}, f32[3,1,4,2,4,128]{5,4,3,2,1,0:T(4,128)S(1)}, u32[]{:S(2)}, u32[]{:S(2)}) collective-permute-start(f32[3,1,4,2,4,128]{5,4,3,2,1,0:T(4,128)S(1)} %constant_dynamic-update-slice_fusion.26), channel_id=1, source_target_pairs={{1,0},{2,1},{3,2},{4,3},{5,4},{6,5},{7,6},{9,8},{10,9},{11,10},{12... | collective-permute-start | bytes 147464 | tf_op jit(solution)/shard_map/ppermute | solution.py:19
  242.1 5.7 %collective-permute-start.18 = (f32[3,1,4,2,4,128]{5,4,3,2,1,0:T(4,128)S(1)}, f32[3,1,4,2,4,128]{5,4,3,2,1,0:T(4,128)S(1)}, u32[]{:S(2)}, u32[]{:S(2)}) collective-permute-start(f32[3,1,4,2,4,128]{5,4,3,2,1,0:T(4,128)S(1)} %constant_dynamic-update-slice_fusion.26), channel_id=1, source_target_pairs={{0,1},{1,2},{2,3},{3,4},{4,5},{5,6},{6,7},{8,9},{9,10},{10,11},{11... | collective-permute-start | bytes 147464 | tf_op jit(solution)/shard_map/ppermute | solution.py:18
  250.6 4.7 %collective-permute-start.20 = (f32[1,1,4,2,4,128]{5,4,3,2,1,0:T(4,128)S(1)}, f32[1,1,4,2,4,128]{5,4,3,2,1,0:T(4,128)S(1)}, u32[]{:S(2)}, u32[]{:S(2)}) collective-permute-start(f32[1,1,4,2,4,128]{5,4,3,2,1,0:T(4,128)S(1)} %copy.108), channel_id=1, source_target_pairs={{0,8},{8,16},{16,24},{1,9},{9,17},{17,25},{2,10},{10,18},{18,26},{... | collective-permute-start | bytes 49160 | tf_op jit(solution)/shard_map/ppermute | solution.py:18
  253.4 5.1 %collective-permute-start.21 = (f32[1,1,4,2,4,128]{5,4,3,2,1,0:T(4,128)S(1)}, f32[1,1,4,2,4,128]{5,4,3,2,1,0:T(4,128)S(1)}, u32[]{:S(2)}, u32[]{:S(2)}) collective-permute-start(f32[1,1,4,2,4,128]{5,4,3,2,1,0:T(4,128)S(1)} %copy.108), channel_id=1, source_target_pairs={{8,0},{16,8},{24,16},{9,1},{17,9},{25,17},{10,2},{18,10},{26,18},{... | collective-permute-start | bytes 49160 | tf_op jit(solution)/shard_map/ppermute | solution.py:19
  258.5 7.6 %collective-permute-start.23 = (f32[3,1,4,2,4,128]{5,4,3,2,1,0:T(4,128)S(1)}, f32[3,1,4,2,4,128]{5,4,3,2,1,0:T(4,128)S(1)}, u32[]{:S(2)}, u32[]{:S(2)}) collective-permute-start(f32[3,1,4,2,4,128]{5,4,3,2,1,0:T(4,128)S(1)} %constant_dynamic-update-slice_fusion.34), channel_id=1, source_target_pairs={{1,0},{2,1},{3,2},{4,3},{5,4},{6,5},{7,6},{9,8},{10,9},{11,10},{12... | collective-permute-start | bytes 147464 | tf_op jit(solution)/shard_map/ppermute | solution.py:19
  259.8 6.3 %collective-permute-start.22 = (f32[3,1,4,2,4,128]{5,4,3,2,1,0:T(4,128)S(1)}, f32[3,1,4,2,4,128]{5,4,3,2,1,0:T(4,128)S(1)}, u32[]{:S(2)}, u32[]{:S(2)}) collective-permute-start(f32[3,1,4,2,4,128]{5,4,3,2,1,0:T(4,128)S(1)} %constant_dynamic-update-slice_fusion.34), channel_id=1, source_target_pairs={{0,1},{1,2},{2,3},{3,4},{4,5},{5,6},{6,7},{8,9},{9,10},{10,11},{11... | collective-permute-start | bytes 147464 | tf_op jit(solution)/shard_map/ppermute | solution.py:18
  270.1 5.6 %collective-permute-start.25 = (f32[1,1,4,4,4,128]{5,4,3,2,1,0:T(4,128)S(1)}, f32[1,1,4,4,4,128]{5,4,3,2,1,0:T(4,128)S(1)}, u32[]{:S(2)}, u32[]{:S(2)}) collective-permute-start(f32[1,1,4,4,4,128]{5,4,3,2,1,0:T(4,128)S(1)} %bitcast.458), channel_id=1, source_target_pairs={{8,0},{16,8},{24,16},{9,1},{17,9},{25,17},{10,2},{18,10},{26,18},{... | collective-permute-start | bytes 98312 | tf_op jit(solution)/shard_map/ppermute | solution.py:19
  272.0 4.7 %collective-permute-start.24 = (f32[1,1,4,4,4,128]{5,4,3,2,1,0:T(4,128)S(1)}, f32[1,1,4,4,4,128]{5,4,3,2,1,0:T(4,128)S(1)}, u32[]{:S(2)}, u32[]{:S(2)}) collective-permute-start(f32[1,1,4,4,4,128]{5,4,3,2,1,0:T(4,128)S(1)} %bitcast.459), channel_id=1, source_target_pairs={{0,8},{8,16},{16,24},{1,9},{9,17},{17,25},{2,10},{10,18},{18,26},{... | collective-permute-start | bytes 98312 | tf_op jit(solution)/shard_map/ppermute | solution.py:18
  276.7 9.7 %collective-permute-start.27 = (f32[3,1,4,4,4,128]{5,4,3,2,1,0:T(4,128)S(1)}, f32[3,1,4,4,4,128]{5,4,3,2,1,0:T(4,128)S(1)}, u32[]{:S(2)}, u32[]{:S(2)}) collective-permute-start(f32[3,1,4,4,4,128]{5,4,3,2,1,0:T(4,128)S(1)} %pad_maximum_fusion.2), channel_id=1, source_target_pairs={{1,0},{2,1},{3,2},{4,3},{5,4},{6,5},{7,6},{9,8},{10,9},{11,10},{12... | collective-permute-start | bytes 294920 | tf_op jit(solution)/shard_map/ppermute | solution.py:19
  278.0 8.3 %collective-permute-start.26 = (f32[3,1,4,4,4,128]{5,4,3,2,1,0:T(4,128)S(1)}, f32[3,1,4,4,4,128]{5,4,3,2,1,0:T(4,128)S(1)}, u32[]{:S(2)}, u32[]{:S(2)}) collective-permute-start(f32[3,1,4,4,4,128]{5,4,3,2,1,0:T(4,128)S(1)} %pad_maximum_fusion.2), channel_id=1, source_target_pairs={{0,1},{1,2},{2,3},{3,4},{4,5},{5,6},{6,7},{8,9},{9,10},{10,11},{11... | collective-permute-start | bytes 294920 | tf_op jit(solution)/shard_map/ppermute | solution.py:18
  295.9 5.8 %collective-permute-start.29 = (f32[1,1,4,4,4,128]{5,4,3,2,1,0:T(4,128)S(1)}, f32[1,1,4,4,4,128]{5,4,3,2,1,0:T(4,128)S(1)}, u32[]{:S(2)}, u32[]{:S(2)}) collective-permute-start(f32[1,1,4,4,4,128]{5,4,3,2,1,0:T(4,128)S(1)} %bitcast.455), channel_id=1, source_target_pairs={{8,0},{16,8},{24,16},{9,1},{17,9},{25,17},{10,2},{18,10},{26,18},{... | collective-permute-start | bytes 98312 | tf_op jit(solution)/shard_map/ppermute | solution.py:19
  298.0 4.7 %collective-permute-start.28 = (f32[1,1,4,4,4,128]{5,4,3,2,1,0:T(4,128)S(1)}, f32[1,1,4,4,4,128]{5,4,3,2,1,0:T(4,128)S(1)}, u32[]{:S(2)}, u32[]{:S(2)}) collective-permute-start(f32[1,1,4,4,4,128]{5,4,3,2,1,0:T(4,128)S(1)} %bitcast.456), channel_id=1, source_target_pairs={{0,8},{8,16},{16,24},{1,9},{9,17},{17,25},{2,10},{10,18},{18,26},{... | collective-permute-start | bytes 98312 | tf_op jit(solution)/shard_map/ppermute | solution.py:18
  302.7 8.7 %collective-permute-start.31 = (f32[3,1,4,4,4,128]{5,4,3,2,1,0:T(4,128)S(1)}, f32[3,1,4,4,4,128]{5,4,3,2,1,0:T(4,128)S(1)}, u32[]{:S(2)}, u32[]{:S(2)}) collective-permute-start(f32[3,1,4,4,4,128]{5,4,3,2,1,0:T(4,128)S(1)} %pad_maximum_fusion.3), channel_id=1, source_target_pairs={{1,0},{2,1},{3,2},{4,3},{5,4},{6,5},{7,6},{9,8},{10,9},{11,10},{12... | collective-permute-start | bytes 294920 | tf_op jit(solution)/shard_map/ppermute | solution.py:19
  304.0 7.4 %collective-permute-start.30 = (f32[3,1,4,4,4,128]{5,4,3,2,1,0:T(4,128)S(1)}, f32[3,1,4,4,4,128]{5,4,3,2,1,0:T(4,128)S(1)}, u32[]{:S(2)}, u32[]{:S(2)}) collective-permute-start(f32[3,1,4,4,4,128]{5,4,3,2,1,0:T(4,128)S(1)} %pad_maximum_fusion.3), channel_id=1, source_target_pairs={{0,1},{1,2},{2,3},{3,4},{4,5},{5,6},{6,7},{8,9},{9,10},{10,11},{11... | collective-permute-start | bytes 294920 | tf_op jit(solution)/shard_map/ppermute | solution.py:18
